TPU v7x, 32 devices: a whole 2x2x4 slice. The times are simulated.
32 devices in a mesh: grp: 2 (over x), gy: 4 (over z), gz: 4 (over y, core).
Axes of the slice: x: 2, y: 2, z: 4, core: 2. Of those that a mesh axis runs over, the one named last changes fastest.
Arguments:
- vorticity: float32 [2, 3, 256, 256, 256], P('grp', None, 'gz', 'gy'), may hold values from -6 to 6
- wind: float32 [2, 3], P('grp'), may hold values from 0.5 to 1.2
Outputs:
- new_vorticity: float32 [2, 3, 256, 256, 256], P('grp', None, 'gz', 'gy')
- velocity: float32 [2, 3, 256, 256, 256], P('grp', None, 'gz', 'gy')
All inputs are finite; a program needn't handle non-finite values.
Results may differ from a plain program's by a relative error of at most 0.0003.
Values sent between devices are 32-bit elements; how exact they have to be, the bound alone decides.
A program may use at most 192 MiB of HBM per device.

v0:
```python
import math

import jax
import jax.numpy as jnp
import numpy as np
from jax import lax
from jax.sharding import PartitionSpec as P

TIME_STEP = 0.4
HIGH = lax.Precision.HIGH


def shifted(value, axis, steps):
    count = lax.axis_size(axis)
    initial, last = (max(0, -steps), min(count, count - steps))
    return lax.ppermute(value, axis, [(source, source + steps) for source in range(initial, last)])


def extended_2(cells, sides, width):
    for axis, dim in sides:
        count = lax.axis_size(axis)
        head = lax.slice_in_dim(cells, 0, width, axis=dim)
        tail = lax.slice_in_dim(cells, cells.shape[dim] - width, cells.shape[dim], axis=dim)
        cells = jnp.concatenate(
            [
                lax.ppermute(tail, axis, [(i, (i + 1) % count) for i in range(count)]),
                cells,
                lax.ppermute(head, axis, [((i + 1) % count, i) for i in range(count)]),
            ],
            axis=dim,
        )
    return cells


def kernel_weight(offset):
    mag = jnp.abs(offset)
    inner = 1.0 - 2.5 * mag * mag + 1.5 * mag * mag * mag
    outer = 0.5 * (2.0 - mag) * (2.0 - mag) * (1.0 - mag)
    return jnp.where(mag < 1.0, inner, jnp.where(mag < 2.0, outer, 0.0 * mag))


def wave_numbers(index, count):
    signed = jnp.where(index < count // 2, index, index - count)
    return signed.astype(jnp.float32) * (2.0 * math.pi / count)


def odd_numbers(index, count):
    signed = jnp.where(index < count // 2, index, index - count)
    signed = jnp.where(index == count // 2, 0 * index, signed)
    return signed.astype(jnp.float32) * (2.0 * math.pi / count)


def curl_of(stream, wave_x, wave_y, wave_z):
    cross_x = wave_y * stream[2] - wave_z * stream[1]
    cross_y = wave_z * stream[0] - wave_x * stream[2]
    cross_z = wave_x * stream[1] - wave_y * stream[0]
    return jnp.stack([cross_x, cross_y, cross_z])


def reversed_lines(values):
    return jnp.roll(jnp.flip(values, (1, 2)), 1, (1, 2))


def curled_pair(real_in, imag_in, scaling, wave_y, wave_z):
    stream_real = real_in * scaling
    stream_imag = imag_in * scaling
    return (-curl_of(stream_imag, 0.0, wave_y, wave_z), curl_of(stream_real, 0.0, wave_y, wave_z))


def exchanged(pieces, axis):
    count = lax.axis_size(axis)
    received = [pieces[0]]
    for step in range(1, count):
        pairs = [(i, (i + step) % count) for i in range(count)]
        received.append(lax.ppermute(pieces[step], axis, pairs))
    return received


def relative(table, dim, axis, sign):
    count = lax.axis_size(axis)
    table = jnp.asarray(table, jnp.float32)
    steps = jnp.arange(count, dtype=jnp.int32)
    order = (lax.axis_index(axis) + sign * steps) % count
    return jnp.take(table, order, axis=dim)


def angles(count):
    positions = np.arange(count)
    product = positions[:, None] * positions[None, :] % count
    angle = product * (2.0 * np.pi / count)
    return (np.cos(angle), np.sin(angle))


def complex_table(count, inverse):
    cosine, sine = angles(count)
    if inverse:
        cosine, sine = (cosine / count, -sine / count)
    rows_real = np.stack([cosine, -sine], 1)
    rows_imag = np.stack([sine, cosine], 1)
    return np.stack([rows_real, rows_imag], 0)


def dot(letters, values, table):
    return jnp.einsum(letters, values, jnp.asarray(table, jnp.float32), precision=HIGH)


def body(vorticity, wind):
    is_wake = lax.axis_index("grp") == 1
    field = vorticity[0]
    drift = wind[0]
    count_x = field.shape[3]
    half_x = count_x // 2
    size_gy = lax.axis_size("gy")
    size_gz = lax.axis_size("gz")
    local_y = field.shape[2]
    count_y = local_y * size_gy
    count_z = field.shape[1] * size_gz
    cosine_x, sine_x = angles(count_x)
    alternate = 1.0 - 2.0 * (np.arange(count_x) % 2)
    forward_cos = cosine_x[:, :half_x]
    forward_sin = np.concatenate([alternate[:, None], -sine_x[:, 1:half_x]], 1)
    cosine_z, sine_z = angles(count_z)
    table_y = complex_table(count_y, False)
    table_y = table_y.reshape(2, size_gy, local_y, 2 * count_y)
    table_y = table_y.transpose(1, 0, 2, 3).reshape(2 * count_y, 2 * count_y)
    owner = lax.axis_index("gy") * size_gz + lax.axis_index("gz")
    share_x = half_x // (size_gy * size_gz)
    local_z = field.shape[1]
    split_x = (count_x, size_gy, size_gz, share_x)
    forward_cos = relative(forward_cos.reshape(split_x), 2, "gz", 1).reshape(count_x, half_x)
    forward_sin = relative(forward_sin.reshape(split_x), 2, "gz", 1).reshape(count_x, half_x)
    split_z = (size_gz, local_z, count_z)
    whole_z = (count_z, count_z)
    forward_z = [relative(t.reshape(split_z), 0, "gz", -1).reshape(whole_z) for t in (cosine_z, sine_z)]
    parts = []
    for comp in range(3):
        lines = jnp.concatenate(
            [
                dot("zyx,xk->kzy", field[comp], forward_cos),
                dot("zyx,xk->kzy", field[comp], forward_sin),
            ],
            2,
        )
        lines = lax.all_to_all(lines, "gy", split_axis=0, concat_axis=2, tiled=True)
        lines = dot("kzl,ln->kzn", lines, table_y)
        pieces = [
            lines[step * share_x : (step + 1) * share_x] for step in range(size_gz)
        ]
        lines = jnp.concatenate(exchanged(pieces, "gz"), 1)
        real_in, imag_in = (lines[..., :count_y], lines[..., count_y:])
        parts.append(
            (
                dot("kzy,zq->kqy", real_in, forward_z[0])
                + dot("kzy,zq->kqy", imag_in, forward_z[1]),
                dot("kzy,zq->kqy", imag_in, forward_z[0])
                - dot("kzy,zq->kqy", real_in, forward_z[1]),
            )
        )
    spectrum = jnp.stack([pair[0] for pair in parts] + [pair[1] for pair in parts])
    local_x = spectrum.shape[1]
    global_x = owner * local_x + jnp.arange(local_x, dtype=jnp.int32)
    index_z = jnp.arange(count_z, dtype=jnp.int32)
    index_y = jnp.arange(count_y, dtype=jnp.int32)
    wave_x = wave_numbers(global_x, count_x)[:, None, None]
    wave_z = wave_numbers(index_z, count_z)[None, :, None]
    wave_y = wave_numbers(index_y, count_y)[None, None, :]
    squared = wave_x * wave_x + wave_y * wave_y + wave_z * wave_z
    inverse = jnp.where(squared > 0, 1.0 / jnp.where(squared > 0, squared, 1.0), 0.0 * squared)
    curl_z = odd_numbers(index_z, count_z)[None, :, None]
    curl_y = odd_numbers(index_y, count_y)[None, None, :]
    stream_real = spectrum[:3] * inverse
    stream_imag = spectrum[3:] * inverse
    curled = jnp.concatenate(
        [
            -curl_of(stream_imag, wave_x, curl_y, curl_z),
            curl_of(stream_real, wave_x, curl_y, curl_z),
        ],
        0,
    )
    packed_plane = spectrum[:, 0]
    plain_real = packed_plane[:3]
    plain_imag = packed_plane[3:]
    mirror_real = reversed_lines(plain_real)
    mirror_imag = reversed_lines(plain_imag)
    base_real = 0.5 * (plain_real + mirror_real)
    base_imag = 0.5 * (plain_imag - mirror_imag)
    top_real = 0.5 * (plain_imag + mirror_imag)
    top_imag = -0.5 * (plain_real - mirror_real)
    plane_squared = wave_z[0] * wave_z[0] + wave_y[0] * wave_y[0]
    base_scale = jnp.where(
        plane_squared > 0,
        1.0 / jnp.where(plane_squared > 0, plane_squared, 1.0),
        0.0 * plane_squared,
    )
    top_scale = 1.0 / (plane_squared + math.pi * math.pi)
    base_vr, base_vi = curled_pair(base_real, base_imag, base_scale, curl_y[0], curl_z[0])
    top_vr, top_vi = curled_pair(top_real, top_imag, top_scale, curl_y[0], curl_z[0])
    rebuilt = jnp.concatenate([base_vr - top_vi, base_vi + top_vr], 0)
    chosen = jnp.where(global_x[0] == 0, rebuilt, curled[:, 0])
    curled = jnp.concatenate([chosen[:, None], curled[:, 1:]], 1)
    back_cos = np.concatenate([cosine_x[:1], 2.0 * cosine_x[1:half_x]], 0) / count_x
    back_sin = np.concatenate([-alternate[None, :], 2.0 * sine_x[1:half_x]], 0) / -count_x
    split_x = (size_gy, size_gz, share_x, count_x)
    back_cos = relative(back_cos.reshape(split_x), 1, "gz", -1).reshape(half_x, count_x)
    back_sin = relative(back_sin.reshape(split_x), 1, "gz", -1).reshape(half_x, count_x)
    split_z = (count_z, size_gz, local_z)
    cosine_z, sine_z = [
        relative(t.reshape(split_z) / count_z, 1, "gz", 1).reshape(whole_z)
        for t in (cosine_z, sine_z)
    ]
    table_y = complex_table(count_y, True)
    table_y = table_y.reshape(2 * count_y, 2, size_gy, local_y)
    table_y = table_y.transpose(2, 0, 1, 3).reshape(size_gy, 2 * count_y, 2 * local_y)
    speeds = []
    for comp in range(3):
        real_in, imag_in = (curled[comp], curled[comp + 3])
        lines = jnp.concatenate(
            [
                dot("kqy,qz->kzy", real_in, cosine_z) - dot("kqy,qz->kzy", imag_in, sine_z),
                dot("kqy,qz->kzy", imag_in, cosine_z) + dot("kqy,qz->kzy", real_in, sine_z),
            ],
            2,
        )
        pieces = [
            lines[:, step * local_z : (step + 1) * local_z] for step in range(size_gz)
        ]
        lines = jnp.concatenate(exchanged(pieces, "gz"), 0)
        lines = jnp.concatenate(
            [dot("kzn,nl->kzl", lines, table_y[side]) for side in range(size_gy)], 0
        )
        lines = lax.all_to_all(lines, "gy", split_axis=0, concat_axis=0, tiled=True)
        speeds.append(
            dot("kzy,kx->zyx", lines[..., :local_y], back_cos)
            + dot("kzy,kx->zyx", lines[..., local_y:], back_sin)
            + drift[comp]
        )
    velocity = jnp.stack(speeds)
    planes = shifted(velocity[..., count_x - 2 :], "grp", 1)
    rimmed = extended_2(velocity, (("gz", 1), ("gy", 2)), 1)
    grad_z = (rimmed[:, 2:, 1:-1, :] - rimmed[:, :-2, 1:-1, :]) * 0.5
    grad_y = (rimmed[:, 1:-1, 2:, :] - rimmed[:, 1:-1, :-2, :]) * 0.5
    left_side = jnp.where(is_wake, planes[..., 1:], velocity[..., count_x - 1 :])
    right_side = jnp.where(is_wake, velocity[..., count_x - 1 :], velocity[..., :1])
    extended = jnp.concatenate([left_side, velocity, right_side], -1)
    grad_x = (extended[..., 2:] - extended[..., :-2]) * 0.5
    strength = field + TIME_STEP * (field[0:1] * grad_x + field[1:2] * grad_y + field[2:3] * grad_z)
    ghost = shifted(strength[..., count_x - 2 :], "grp", 1)
    shift_x = TIME_STEP * velocity[0]
    left_q = jnp.where(is_wake, ghost, strength[..., count_x - 2 :])
    left_d = jnp.where(is_wake, TIME_STEP * planes[0], shift_x[..., count_x - 2 :])
    right_q = jnp.where(is_wake, 0.0, strength[..., :2])
    right_d = jnp.where(is_wake, 0.0, shift_x[..., :2])
    q_ext = jnp.concatenate([left_q, strength, right_q], -1)
    d_ext = jnp.concatenate([left_d, shift_x, right_d], -1)
    moved = jnp.zeros_like(strength)
    for offset in range(-2, 3):
        start = 2 - offset
        moved = moved + q_ext[..., start : start + count_x] * kernel_weight(
            offset - d_ext[..., start : start + count_x]
        )
    packed = jnp.concatenate([moved, TIME_STEP * velocity[1:2]], 0)
    rim_rows = extended_2(packed, (("gy", 2),), 2)
    width_y = moved.shape[2]
    lateral = jnp.zeros_like(moved)
    for offset in range(-2, 3):
        start = 2 - offset
        lateral = lateral + rim_rows[:3, :, start : start + width_y, :] * kernel_weight(
            offset - rim_rows[3:4, :, start : start + width_y, :]
        )
    packed = jnp.concatenate([lateral, TIME_STEP * velocity[2:3]], 0)
    rim_cols = extended_2(packed, (("gz", 1),), 2)
    width_z = moved.shape[1]
    result = jnp.zeros_like(moved)
    for offset in range(-2, 3):
        start = 2 - offset
        result = result + rim_cols[:3, start : start + width_z, :, :] * kernel_weight(
            offset - rim_cols[3:4, start : start + width_z, :, :]
        )
    return (result[None], velocity[None])


def solution(mesh):
    return jax.shard_map(
        body,
        mesh=mesh,
        in_specs=(P("grp", None, "gz", "gy", None), P("grp", None)),
        out_specs=(P("grp", None, "gz", "gy", None), P("grp", None, "gz", "gy", None)),
        check_vma=False,
    )
```

profile of v0, /device:TPU:0, one launch (start us, length us, event | category | flops | bytes accessed | tf_op | source)
XLA Modules:
  0.0 1232.2 jit_solution(4995639777925526722)
XLA Ops:
  41.1 77.6 %all-to-all-done = f32[128,64,128]{2,1,0:T(8,128)} async-done(((f32[128,64,128]{2,1,0:T(8,128)}), f32[128,64,128]{2,1,0:T(8,128)}, u32[]{:S(2)}, u32[]{:S(2)}) %all-to-all-start) | async-done | bytes 4194336 | tf_op jit(solution)/shard_map/all_to_all | solution.py:144
  139.6 76.8 %all-to-all-done.1 = f32[128,64,128]{2,1,0:T(8,128)} async-done(((f32[128,64,128]{2,1,0:T(8,128)}), f32[128,64,128]{2,1,0:T(8,128)}, u32[]{:S(2)}, u32[]{:S(2)}) %all-to-all-start.1) | async-done | bytes 4194336 | tf_op jit(solution)/shard_map/all_to_all | solution.py:144
  244.7 11.4 collective-permute-done
  256.4 57.6 %all-to-all-done.2 = f32[128,64,128]{2,1,0:T(8,128)} async-done(((f32[128,64,128]{2,1,0:T(8,128)}), f32[128,64,128]{2,1,0:T(8,128)}, u32[]{:S(2)}, u32[]{:S(2)}) %all-to-all-start.2) | async-done | bytes 4194336 | tf_op jit(solution)/shard_map/all_to_all | solution.py:144
  332.6 13.3 %collective-permute-done.6 = f32[8,64,512]{2,1,0:T(8,128)S(1)} collective-permute-done((f32[8,64,512]{2,1,0:T(8,128)S(1)}, f32[8,64,512]{2,1,0:T(8,128)S(1)}, u32[]{:S(2)}, u32[]{:S(2)}) %collective-permute-start.6) | collective-permute-done | bytes 1048608 | tf_op jit(solution)/shard_map/ppermute | solution.py:75
  349.4 19.8 %collective-permute-done.8 = f32[8,64,512]{2,1,0:T(8,128)S(1)} collective-permute-done((f32[8,64,512]{2,1,0:T(8,128)S(1)}, f32[8,64,512]{2,1,0:T(8,128)S(1)}, u32[]{:S(2)}, u32[]{:S(2)}) %collective-permute-start.8) | collective-permute-done | bytes 1048608 | tf_op jit(solution)/shard_map/ppermute | solution.py:75
  432.2 14.5 %collective-permute-done.9 = f32[8,64,512]{2,1,0:T(8,128)} collective-permute-done((f32[8,64,512]{2,1,0:T(8,128)}, f32[8,64,512]{2,1,0:T(8,128)}, u32[]{:S(2)}, u32[]{:S(2)}) %collective-permute-start.9) | collective-permute-done | bytes 1048608 | tf_op jit(solution)/shard_map/ppermute | solution.py:75
  458.6 13.0 %collective-permute-done.11 = f32[8,64,512]{2,1,0:T(8,128)} collective-permute-done((f32[8,64,512]{2,1,0:T(8,128)}, f32[8,64,512]{2,1,0:T(8,128)}, u32[]{:S(2)}, u32[]{:S(2)}) %collective-permute-start.11) | collective-permute-done | bytes 1048608 | tf_op jit(solution)/shard_map/ppermute | solution.py:75
  474.8 9.7 fusion.268
  540.6 12.6 %collective-permute-done.12 = f32[8,64,512]{2,1,0:T(8,128)} collective-permute-done((f32[8,64,512]{2,1,0:T(8,128)}, f32[8,64,512]{2,1,0:T(8,128)}, u32[]{:S(2)}, u32[]{:S(2)}) %collective-permute-start.12) | collective-permute-done | bytes 1048608 | tf_op jit(solution)/shard_map/ppermute | solution.py:75
  555.1 8.9 collective-permute-done.13
  567.1 13.0 %collective-permute-done.14 = f32[8,64,512]{2,1,0:T(8,128)} collective-permute-done((f32[8,64,512]{2,1,0:T(8,128)}, f32[8,64,512]{2,1,0:T(8,128)}, u32[]{:S(2)}, u32[]{:S(2)}) %collective-permute-start.14) | collective-permute-done | bytes 1048608 | tf_op jit(solution)/shard_map/ppermute | solution.py:75
  583.3 9.7 fusion.264
  647.6 14.1 %collective-permute-done.15 = f32[8,64,512]{2,1,0:T(8,128)} collective-permute-done((f32[8,64,512]{2,1,0:T(8,128)S(1)}, f32[8,64,512]{2,1,0:T(8,128)}, u32[]{:S(2)}, u32[]{:S(2)}) %collective-permute-start.15) | collective-permute-done | bytes 1048608 | tf_op jit(solution)/shard_map/ppermute | solution.py:75
  673.9 12.8 %collective-permute-done.17 = f32[8,64,512]{2,1,0:T(8,128)} collective-permute-done((f32[8,64,512]{2,1,0:T(8,128)}, f32[8,64,512]{2,1,0:T(8,128)}, u32[]{:S(2)}, u32[]{:S(2)}) %collective-permute-start.17) | collective-permute-done | bytes 1048608 | tf_op jit(solution)/shard_map/ppermute | solution.py:75
  689.9 9.7 fusion.260
  729.8 10.1 bitcast_multiply_fusion.2
  768.5 52.8 %all-to-all-done.5 = f32[128,64,128]{2,1,0:T(8,128)} async-done(((f32[128,64,128]{2,1,0:T(8,128)}), f32[128,64,128]{2,1,0:T(8,128)}, u32[]{:S(2)}, u32[]{:S(2)}) %all-to-all-start.5) | async-done | bytes 4194336 | tf_op jit(solution)/shard_map/all_to_all | solution.py:231
  845.4 12.2 fusion.42
  895.6 12.8 %slice_select_fusion.1 = (f32[3,64,64,1]{3,2,1,0:T(8,128)}, f32[3,64,64,1]{3,2,1,0:T(8,128)}) fusion(f32[3,64,64,256]{3,2,1,0:T(8,128)} %copy-done.5, pred[]{:T(512)S(6)} %eq.87, f32[3,64,64,1]{3,2,1,0:T(8,128)} %copy.335), kind=kLoop, calls=%fused_computation.87 | loop fusion | flops 24576 | bytes 245761 | tf_op jit(solution)/shard_map/jit(_where)/select_n | solution.py:243
  924.0 48.6 %fusion.23 = f32[3,64,64,256]{3,2,1,0:T(8,128)} fusion(f32[3,1,64,256]{3,2,1,0:T(8,128)S(1)} %collective-permute-done.19, f32[1,64,64,256]{3,2,1,0:T(8,128)} %bitcast.339, f32[1,64,64,256]{3,2,1,0:T(8,128)} %bitcast.342, f32[1,64,64,256]{3,2,1,0:T(8,128)} %bitcast.345, f32[3,1,64,256]{3,2,1,0:T(8,128)S(1)} %collective-permute-done.20, ...), kind=kLoop, calls=%fused_computation.50 | loop fusion | flops 100663296 | bytes 51228672 | tf_op jit(solution)/shard_map/add | solution.py:246
  990.4 19.7 %fusion.32 = (f32[64,64,256]{2,1,0:T(8,128)}, f32[64,64,256]{2,1,0:T(8,128)}, f32[64,64,256]{2,1,0:T(8,128)}, f32[64,64,256]{2,1,0:T(8,128)}) fusion(f32[64,64,2]{2,1,0:T(8,128)S(1)} %get-tuple-element.62, f32[64,64,256]{2,1,0:T(8,128)} %get-tuple-element.65, f32[64,64,2]{2,1,0:T(8,128)} %get-tuple-element.63), kind=kLoop, calls=%fused_computation.161 | loop fusion | flops 83886080 | bytes 21037056 | tf_op jit(solution)/shard_map/jit(_where)/select_n | solution.py:39
  1014.3 11.5 slice_select_fusion
  1025.8 41.5 %fusion.3 = f32[3,64,64,256]{3,2,1,0:T(8,128)} fusion(f32[3,64,64,2]{3,2,1,0:T(8,128)} %get-tuple-element.31, f32[3,64,64,256]{3,2,1,0:T(8,128)} %fusion.23, f32[3,64,64,2]{3,2,1,0:T(8,128)} %get-tuple-element.30, f32[64,64,256]{2,1,0:T(8,128)} %get-tuple-element.60, f32[64,64,256]{2,1,0:T(8,128)} %get-tuple-element.61, ...), kind=kLoop, calls=%fused_computation.19 | loop fusion | flops 40894464 | bytes 46333952 | tf_op jit(solution)/shard_map/add | solution.py:258
  1084.2 11.0 collective-permute-done.25
  1095.2 13.1 %fusion.58 = (f32[64,64,256]{2,1,0:T(8,128)}, f32[64,64,256]{2,1,0:T(8,128)}, f32[64,64,256]{2,1,0:T(8,128)}, f32[64,64,256]{2,1,0:T(8,128)}) fusion(f32[4,64,2,256]{3,2,1,0:T(2,128)S(1)} %collective-permute-done.24, f32[1,64,64,256]{3,2,1,0:T(8,128)S(1)} %copy-done.7, f32[3,64,64,256]{3,2,1,0:T(8,128)S(1)} %bitcast.336, ...), kind=kLoop, calls=%fused_computation.187 | loop fusion | flops 88080384 | bytes 34603008 | tf_op jit(solution)/shard_map/mul | solution.py:267
  1108.3 13.1 %pad_maximum_fusion = (f32[4,64,66,256]{3,2,1,0:T(8,128)}, f32[4,64,66,256]{3,2,1,0:T(8,128)}) fusion(f32[4,64,2,256]{3,2,1,0:T(2,128)S(1)} %collective-permute-done.24, f32[1,64,64,256]{3,2,1,0:T(8,128)S(1)} %copy-done.7, f32[3,64,64,256]{3,2,1,0:T(8,128)S(1)} %bitcast.336, f32[4,64,2,256]{3,2,1,0:T(2,128)S(1)} %collective-permute-done.25), kind=kLoop, calls=%fused_computation.12 | loop fusion | flops 17301504 | bytes 52428800 | tf_op jit(solution)/shard_map/concatenate | solution.py:24
  1121.3 34.0 %fusion.13 = f32[3,64,64,256]{3,2,1,0:T(8,128)} fusion(f32[4,64,66,256]{3,2,1,0:T(8,128)} %get-tuple-element.23, f32[4,64,66,256]{3,2,1,0:T(8,128)} %get-tuple-element.22, f32[3,64,64,256]{3,2,1,0:T(8,128)} %fusion.3, f32[64,64,256]{2,1,0:T(8,128)} %get-tuple-element.20, f32[64,64,256]{2,1,0:T(8,128)} %get-tuple-element.21, ...), kind=kLoop, calls=%fused_computation.34 | loop fusion | flops 28311552 | bytes 96468992 | tf_op jit(solution)/shard_map/add | solution.py:267
  1157.6 10.7 collective-permute-done.26
  1171.6 11.6 fusion.87
  1183.3 15.5 %pad_maximum_fusion.1 = (f32[4,66,64,256]{3,2,1,0:T(8,128)}, f32[4,66,64,256]{3,2,1,0:T(8,128)}) fusion(f32[4,2,64,256]{3,2,1,0:T(8,128)} %copy-done.24, f32[1,64,64,256]{3,2,1,0:T(8,128)} %get-tuple-element.57, f32[3,64,64,256]{3,2,1,0:T(8,128)S(1)} %copy-done, f32[4,2,64,256]{3,2,1,0:T(8,128)} %copy-done.25), kind=kLoop, calls=%fused_computation.14 | loop fusion | flops 17301504 | bytes 52428800 | tf_op jit(solution)/shard_map/concatenate | solution.py:24
  1198.8 33.0 %fusion.9 = f32[1,3,64,64,256]{4,3,2,1,0:T(8,128)} fusion(f32[4,66,64,256]{3,2,1,0:T(8,128)} %get-tuple-element.17, f32[4,66,64,256]{3,2,1,0:T(8,128)} %get-tuple-element.16, f32[3,64,64,256]{3,2,1,0:T(8,128)} %fusion.13, f32[64,64,256]{2,1,0:T(8,128)} %get-tuple-element.14, f32[64,64,256]{2,1,0:T(8,128)} %get-tuple-element.15, ...), kind=kLoop, calls=%fused_computation.26 | loop fusion | flops 28311552 | bytes 96468992 | tf_op jit(solution)/shard_map/broadcast_in_dim | solution.py:279
  (323 shorter events, 504.1 us)
Async XLA Ops:
  18.8 99.8 %all-to-all-start = ((f32[128,64,128]{2,1,0:T(8,128)}), f32[128,64,128]{2,1,0:T(8,128)}, u32[]{:S(2)}, u32[]{:S(2)}) async-start(f32[128,64,128]{2,1,0:T(8,128)} %copy.238), calls=%async_computation | async-start | bytes 8388608 | tf_op jit(solution)/shard_map/all_to_all | solution.py:144
  118.6 97.8 %all-to-all-start.1 = ((f32[128,64,128]{2,1,0:T(8,128)}), f32[128,64,128]{2,1,0:T(8,128)}, u32[]{:S(2)}, u32[]{:S(2)}) async-start(f32[128,64,128]{2,1,0:T(8,128)} %copy.244), calls=%async_computation.1 | async-start | bytes 8388608 | tf_op jit(solution)/shard_map/all_to_all | solution.py:144
  216.4 97.6 %all-to-all-start.2 = ((f32[128,64,128]{2,1,0:T(8,128)}), f32[128,64,128]{2,1,0:T(8,128)}, u32[]{:S(2)}, u32[]{:S(2)}) async-start(f32[128,64,128]{2,1,0:T(8,128)} %copy.250), calls=%async_computation.2 | async-start | bytes 8388608 | tf_op jit(solution)/shard_map/all_to_all | solution.py:144
  232.3 23.7 %collective-permute-start = (f32[8,64,512]{2,1,0:T(8,128)S(1)}, f32[8,64,512]{2,1,0:T(8,128)}, u32[]{:S(2)}, u32[]{:S(2)}) collective-permute-start(f32[8,64,512]{2,1,0:T(8,128)S(1)} %get-tuple-element.87), channel_id=1, source_target_pairs={{0,1},{1,2},{2,3},{3,0},{4,5},{5,6},{6,7},{7,4},{8,9},{9,10},{10,1... | collective-permute-start | bytes 3145736 | tf_op jit(solution)/shard_map/ppermute | solution.py:75
  233.4 87.1 %collective-permute-start.1 = (f32[8,64,512]{2,1,0:T(8,128)}, f32[8,64,512]{2,1,0:T(8,128)}, u32[]{:S(2)}, u32[]{:S(2)}) collective-permute-start(f32[8,64,512]{2,1,0:T(8,128)} %get-tuple-element.86), channel_id=1, source_target_pairs={{0,2},{1,3},{2,0},{3,1},{4,6},{5,7},{6,4},{7,5},{8,10},{9,11},{10,... | collective-permute-start | bytes 3145736 | tf_op jit(solution)/shard_map/ppermute | solution.py:75
  234.9 85.6 %collective-permute-start.2 = (f32[8,64,512]{2,1,0:T(8,128)}, f32[8,64,512]{2,1,0:T(8,128)}, u32[]{:S(2)}, u32[]{:S(2)}) collective-permute-start(f32[8,64,512]{2,1,0:T(8,128)} %get-tuple-element.85), channel_id=1, source_target_pairs={{0,3},{1,0},{2,1},{3,2},{4,7},{5,4},{6,5},{7,6},{8,11},{9,8},{10,9... | collective-permute-start | bytes 3145736 | tf_op jit(solution)/shard_map/ppermute | solution.py:75
  244.2 81.4 %collective-permute-start.3 = (f32[8,64,512]{2,1,0:T(8,128)}, f32[8,64,512]{2,1,0:T(8,128)}, u32[]{:S(2)}, u32[]{:S(2)}) collective-permute-start(f32[8,64,512]{2,1,0:T(8,128)} %get-tuple-element.91), channel_id=1, source_target_pairs={{0,1},{1,2},{2,3},{3,0},{4,5},{5,6},{6,7},{7,4},{8,9},{9,10},{10,1... | collective-permute-start | bytes 3145736 | tf_op jit(solution)/shard_map/ppermute | solution.py:75
  244.2 82.8 %collective-permute-start.4 = (f32[8,64,512]{2,1,0:T(8,128)}, f32[8,64,512]{2,1,0:T(8,128)}, u32[]{:S(2)}, u32[]{:S(2)}) collective-permute-start(f32[8,64,512]{2,1,0:T(8,128)} %get-tuple-element.90), channel_id=1, source_target_pairs={{0,2},{1,3},{2,0},{3,1},{4,6},{5,7},{6,4},{7,5},{8,10},{9,11},{10,... | collective-permute-start | bytes 3145736 | tf_op jit(solution)/shard_map/ppermute | solution.py:75
  256.0 71.0 %collective-permute-start.5 = (f32[8,64,512]{2,1,0:T(8,128)}, f32[8,64,512]{2,1,0:T(8,128)}, u32[]{:S(2)}, u32[]{:S(2)}) collective-permute-start(f32[8,64,512]{2,1,0:T(8,128)} %get-tuple-element.89), channel_id=1, source_target_pairs={{0,3},{1,0},{2,1},{3,2},{4,7},{5,4},{6,5},{7,6},{8,11},{9,8},{10,9... | collective-permute-start | bytes 3145736 | tf_op jit(solution)/shard_map/ppermute | solution.py:75
  320.4 25.5 %collective-permute-start.6 = (f32[8,64,512]{2,1,0:T(8,128)S(1)}, f32[8,64,512]{2,1,0:T(8,128)S(1)}, u32[]{:S(2)}, u32[]{:S(2)}) collective-permute-start(f32[8,64,512]{2,1,0:T(8,128)S(1)} %get-tuple-element.95), channel_id=1, source_target_pairs={{0,1},{1,2},{2,3},{3,0},{4,5},{5,6},{6,7},{7,4},{8,9},{9,10},{10,1... | collective-permute-start | bytes 3145736 | tf_op jit(solution)/shard_map/ppermute | solution.py:75
  320.5 28.8 %collective-permute-start.7 = (f32[8,64,512]{2,1,0:T(8,128)S(1)}, f32[8,64,512]{2,1,0:T(8,128)S(1)}, u32[]{:S(2)}, u32[]{:S(2)}) collective-permute-start(f32[8,64,512]{2,1,0:T(8,128)S(1)} %get-tuple-element.94), channel_id=1, source_target_pairs={{0,2},{1,3},{2,0},{3,1},{4,6},{5,7},{6,4},{7,5},{8,10},{9,11},{10,... | collective-permute-start | bytes 3145736 | tf_op jit(solution)/shard_map/ppermute | solution.py:75
  325.5 43.6 %collective-permute-start.8 = (f32[8,64,512]{2,1,0:T(8,128)S(1)}, f32[8,64,512]{2,1,0:T(8,128)S(1)}, u32[]{:S(2)}, u32[]{:S(2)}) collective-permute-start(f32[8,64,512]{2,1,0:T(8,128)S(1)} %get-tuple-element.93), channel_id=1, source_target_pairs={{0,3},{1,0},{2,1},{3,2},{4,7},{5,4},{6,5},{7,6},{8,11},{9,8},{10,9... | collective-permute-start | bytes 3145736 | tf_op jit(solution)/shard_map/ppermute | solution.py:75
  425.1 21.6 %collective-permute-start.9 = (f32[8,64,512]{2,1,0:T(8,128)}, f32[8,64,512]{2,1,0:T(8,128)}, u32[]{:S(2)}, u32[]{:S(2)}) collective-permute-start(f32[8,64,512]{2,1,0:T(8,128)} %copy.280), channel_id=1, source_target_pairs={{0,1},{1,2},{2,3},{3,0},{4,5},{5,6},{6,7},{7,4},{8,9},{9,10},{10,1... | collective-permute-start | bytes 3145736 | tf_op jit(solution)/shard_map/ppermute | solution.py:75
  429.1 26.3 %collective-permute-start.10 = (f32[8,64,512]{2,1,0:T(8,128)}, f32[8,64,512]{2,1,0:T(8,128)}, u32[]{:S(2)}, u32[]{:S(2)}) collective-permute-start(f32[8,64,512]{2,1,0:T(8,128)} %copy.281), channel_id=1, source_target_pairs={{0,2},{1,3},{2,0},{3,1},{4,6},{5,7},{6,4},{7,5},{8,10},{9,11},{10,... | collective-permute-start | bytes 3145736 | tf_op jit(solution)/shard_map/ppermute | solution.py:75
  432.2 39.4 %collective-permute-start.11 = (f32[8,64,512]{2,1,0:T(8,128)}, f32[8,64,512]{2,1,0:T(8,128)}, u32[]{:S(2)}, u32[]{:S(2)}) collective-permute-start(f32[8,64,512]{2,1,0:T(8,128)} %copy.282), channel_id=1, source_target_pairs={{0,3},{1,0},{2,1},{3,2},{4,7},{5,4},{6,5},{7,6},{8,11},{9,8},{10,9... | collective-permute-start | bytes 3145736 | tf_op jit(solution)/shard_map/ppermute | solution.py:75
  507.3 108.5 %all-to-all-start.3 = ((f32[128,64,128]{2,1,0:T(8,128)}), f32[128,64,128]{2,1,0:T(8,128)}, u32[]{:S(2)}, u32[]{:S(2)}) async-start(f32[128,64,128]{2,1,0:T(8,128)} %pad_maximum_fusion.40), calls=%async_computation.3 | async-start | bytes 8388608 | tf_op jit(solution)/shard_map/all_to_all | solution.py:231
  532.8 20.4 %collective-permute-start.12 = (f32[8,64,512]{2,1,0:T(8,128)}, f32[8,64,512]{2,1,0:T(8,128)}, u32[]{:S(2)}, u32[]{:S(2)}) collective-permute-start(f32[8,64,512]{2,1,0:T(8,128)} %copy.302), channel_id=1, source_target_pairs={{0,1},{1,2},{2,3},{3,0},{4,5},{5,6},{6,7},{7,4},{8,9},{9,10},{10,1... | collective-permute-start | bytes 3145736 | tf_op jit(solution)/shard_map/ppermute | solution.py:75
  537.6 26.3 %collective-permute-start.13 = (f32[8,64,512]{2,1,0:T(8,128)}, f32[8,64,512]{2,1,0:T(8,128)}, u32[]{:S(2)}, u32[]{:S(2)}) collective-permute-start(f32[8,64,512]{2,1,0:T(8,128)} %copy.303), channel_id=1, source_target_pairs={{0,2},{1,3},{2,0},{3,1},{4,6},{5,7},{6,4},{7,5},{8,10},{9,11},{10,... | collective-permute-start | bytes 3145736 | tf_op jit(solution)/shard_map/ppermute | solution.py:75
  539.7 40.4 %collective-permute-start.14 = (f32[8,64,512]{2,1,0:T(8,128)}, f32[8,64,512]{2,1,0:T(8,128)}, u32[]{:S(2)}, u32[]{:S(2)}) collective-permute-start(f32[8,64,512]{2,1,0:T(8,128)} %copy.304), channel_id=1, source_target_pairs={{0,3},{1,0},{2,1},{3,2},{4,7},{5,4},{6,5},{7,6},{8,11},{9,8},{10,9... | collective-permute-start | bytes 3145736 | tf_op jit(solution)/shard_map/ppermute | solution.py:75
  615.8 106.7 %all-to-all-start.4 = ((f32[128,64,128]{2,1,0:T(8,128)}), f32[128,64,128]{2,1,0:T(8,128)}, u32[]{:S(2)}, u32[]{:S(2)}) async-start(f32[128,64,128]{2,1,0:T(8,128)} %pad_maximum_fusion.41), calls=%async_computation.4 | async-start | bytes 8388608 | tf_op jit(solution)/shard_map/all_to_all | solution.py:231
  640.3 21.3 %collective-permute-start.15 = (f32[8,64,512]{2,1,0:T(8,128)S(1)}, f32[8,64,512]{2,1,0:T(8,128)}, u32[]{:S(2)}, u32[]{:S(2)}) collective-permute-start(f32[8,64,512]{2,1,0:T(8,128)S(1)} %copy.322), channel_id=1, source_target_pairs={{0,1},{1,2},{2,3},{3,0},{4,5},{5,6},{6,7},{7,4},{8,9},{9,10},{10,1... | collective-permute-start | bytes 3145736 | tf_op jit(solution)/shard_map/ppermute | solution.py:75
  644.4 26.3 %collective-permute-start.16 = (f32[8,64,512]{2,1,0:T(8,128)}, f32[8,64,512]{2,1,0:T(8,128)}, u32[]{:S(2)}, u32[]{:S(2)}) collective-permute-start(f32[8,64,512]{2,1,0:T(8,128)} %copy.323), channel_id=1, source_target_pairs={{0,2},{1,3},{2,0},{3,1},{4,6},{5,7},{6,4},{7,5},{8,10},{9,11},{10,... | collective-permute-start | bytes 3145736 | tf_op jit(solution)/shard_map/ppermute | solution.py:75
  647.6 39.1 %collective-permute-start.17 = (f32[8,64,512]{2,1,0:T(8,128)}, f32[8,64,512]{2,1,0:T(8,128)}, u32[]{:S(2)}, u32[]{:S(2)}) collective-permute-start(f32[8,64,512]{2,1,0:T(8,128)} %copy.324), channel_id=1, source_target_pairs={{0,3},{1,0},{2,1},{3,2},{4,7},{5,4},{6,5},{7,6},{8,11},{9,8},{10,9... | collective-permute-start | bytes 3145736 | tf_op jit(solution)/shard_map/ppermute | solution.py:75
  722.5 98.8 %all-to-all-start.5 = ((f32[128,64,128]{2,1,0:T(8,128)}), f32[128,64,128]{2,1,0:T(8,128)}, u32[]{:S(2)}, u32[]{:S(2)}) async-start(f32[128,64,128]{2,1,0:T(8,128)} %pad_maximum_fusion.42), calls=%async_computation.5 | async-start | bytes 8388608 | tf_op jit(solution)/shard_map/all_to_all | solution.py:231
  887.4 23.0 %collective-permute-start.19 = (f32[3,1,64,256]{3,2,1,0:T(8,128)S(1)}, f32[3,1,64,256]{3,2,1,0:T(8,128)S(1)}, u32[]{:S(2)}, u32[]{:S(2)}) collective-permute-start(f32[3,1,64,256]{3,2,1,0:T(8,128)S(1)} %get-tuple-element.38), channel_id=1, source_target_pairs={{0,1},{1,2},{2,3},{3,0},{4,5},{5,6},{6,7},{7,4},{8,9},{9,10},{10,1... | collective-permute-start | bytes 589832 | tf_op jit(solution)/shard_map/ppermute | solution.py:26
  888.0 22.4 %collective-permute-start.20 = (f32[3,1,64,256]{3,2,1,0:T(8,128)S(1)}, f32[3,1,64,256]{3,2,1,0:T(8,128)S(1)}, u32[]{:S(2)}, u32[]{:S(2)}) collective-permute-start(f32[3,1,64,256]{3,2,1,0:T(8,128)S(1)} %get-tuple-element.37), channel_id=1, source_target_pairs={{1,0},{2,1},{3,2},{0,3},{5,4},{6,5},{7,6},{4,7},{9,8},{10,9},{11,1... | collective-permute-start | bytes 589832 | tf_op jit(solution)/shard_map/ppermute | solution.py:28
  912.7 11.3 collective-permute-start.21
  984.2 26.0 %collective-permute-start.23 = (f32[3,64,64,2]{2,1,3,0:T(8,128)S(1)}, f32[3,64,64,2]{2,1,3,0:T(8,128)S(1)}, u32[]{:S(2)}, u32[]{:S(2)}) collective-permute-start(f32[3,64,64,2]{2,1,3,0:T(8,128)S(1)} %copy.336), channel_id=1, source_target_pairs={{0,16},{1,17},{2,18},{3,19},{4,20},{5,21},{6,22},{7,23},{8,24},{9,... | collective-permute-start | bytes 294920 | tf_op jit(solution)/shard_map/ppermute | solution.py:16
  1070.0 14.1 %collective-permute-start.24 = (f32[4,64,2,256]{3,2,1,0:T(2,128)S(1)}, f32[4,64,2,256]{3,2,1,0:T(2,128)S(1)}, u32[]{:S(2)}, u32[]{:S(2)}) collective-permute-start(f32[4,64,2,256]{3,2,1,0:T(2,128)S(1)} %get-tuple-element.24), channel_id=1, source_target_pairs={{4,0},{8,4},{12,8},{0,12},{5,1},{9,5},{13,9},{1,13},{6,2},{10,6},{... | collective-permute-start | bytes 1572872 | tf_op jit(solution)/shard_map/ppermute | solution.py:28
  1071.8 23.3 %collective-permute-start.25 = (f32[4,64,2,256]{3,2,1,0:T(2,128)S(1)}, f32[4,64,2,256]{3,2,1,0:T(2,128)S(1)}, u32[]{:S(2)}, u32[]{:S(2)}) collective-permute-start(f32[4,64,2,256]{3,2,1,0:T(2,128)S(1)} %get-tuple-element.25), channel_id=1, source_target_pairs={{0,4},{4,8},{8,12},{12,0},{1,5},{5,9},{9,13},{13,1},{2,6},{6,10},{... | collective-permute-start | bytes 1572872 | tf_op jit(solution)/shard_map/ppermute | solution.py:26
  1156.8 11.5 collective-permute-start.26
  1156.9 13.9 %collective-permute-start.27 = (f32[4,2,64,256]{3,2,1,0:T(8,128)S(1)}, f32[4,2,64,256]{3,2,1,0:T(8,128)S(1)}, u32[]{:S(2)}, u32[]{:S(2)}) collective-permute-start(f32[4,2,64,256]{3,2,1,0:T(8,128)S(1)} %get-tuple-element.19), channel_id=1, source_target_pairs={{0,1},{1,2},{2,3},{3,0},{4,5},{5,6},{6,7},{7,4},{8,9},{9,10},{10,1... | collective-permute-start | bytes 1572872 | tf_op jit(solution)/shard_map/ppermute | solution.py:26
  (59 other events, 1078.8 us)
where the time goes:
time: 1240 us; the launch traced here: 1230 us
  waiting for transfers between devices  456 us (37%)
  other arithmetic  339 us (27%)
  matrix products  223 us (18%)
  local copies, waits for them, and re-layouts  148 us (12%)
  starting transfers between devices  63 us (5%)
    dot_general x51, matrix products, dot(): jnp.einsum(letters, values, jnp.asarray(table, jnp.float32), precision=HIGH)  223 us
    all_to_all x3, waiting for transfers between devices, body(): lines = lax.all_to_all(lines, 'gy', split_axis=0, concat_axis=2, tiled=True)  212 us
    ppermute x18, waiting for transfers between devices, exchanged(): received.append(lax.ppermute(pieces[step], axis, pairs))  151 us
    all_to_all x3, waiting for transfers between devices, body(): lines = lax.all_to_all(lines, 'gy', split_axis=0, concat_axis=0, tiled=True)  52.8 us
    add x1, other arithmetic, body(): field + TIME_STEP * (field[0:1] * grad_x + field[1:2] * grad_y + field[2:...  48.6 us
    add x1, other arithmetic, body(): moved + q_ext[..., start:start + count_x] * kernel_weight(offset - d_ext[...  41.5 us
    broadcast_in_dim x2, other arithmetic, body(): return (result[None], velocity[None])  38.8 us
    add x1, other arithmetic, body(): lateral + rim_rows[:3, :, start:start + width_y, :] * kernel_weight(offse...  34 us
  transfers between devices with their start and end apart: 34, of which 23 were waited for; matrix products, arithmetic and copies ran while one was open for 24% of the time, Pallas kernels for 0%

commit v1 on v0

v1 whole, which is shorter than its diff:
```python
import functools
import math

import jax
import jax.numpy as jnp
import numpy as np
from jax import lax
from jax.experimental import pallas as pl
from jax.experimental.pallas import tpu as pltpu
from jax.sharding import PartitionSpec as P

TIME_STEP = 0.4
HIGH = lax.Precision.HIGH
BF16 = jnp.bfloat16
F32 = jnp.float32
VMEM_BYTES = 56 * 1024 * 1024
COLUMNS = 16


def shifted(value, axis, steps):
    count = lax.axis_size(axis)
    initial, last = (max(0, -steps), min(count, count - steps))
    return lax.ppermute(value, axis, [(source, source + steps) for source in range(initial, last)])


def rims(cells, axis, dim, width):
    count = lax.axis_size(axis)
    head = lax.slice_in_dim(cells, 0, width, axis=dim)
    tail = lax.slice_in_dim(cells, cells.shape[dim] - width, cells.shape[dim], axis=dim)
    low = lax.ppermute(tail, axis, [(i, (i + 1) % count) for i in range(count)])
    high = lax.ppermute(head, axis, [((i + 1) % count, i) for i in range(count)])
    return low, high


def rimmed(cells, sides, width):
    for axis, dim in sides:
        low, high = rims(cells, axis, dim, width)
        cells = jnp.concatenate([low, cells, high], axis=dim)
    return cells


def kernel_weight(offset):
    mag = jnp.abs(offset)
    inner = 1.0 - 2.5 * mag * mag + 1.5 * mag * mag * mag
    outer = 0.5 * (2.0 - mag) * (2.0 - mag) * (1.0 - mag)
    return jnp.where(mag < 1.0, inner, jnp.where(mag < 2.0, outer, 0.0 * mag))


def double_weight(offset):
    e = jnp.maximum(1.0 - jnp.abs(offset), -1.0)
    u = 1.0 + e
    p = jnp.maximum(e, 0.0)
    return u * u * e + p * p * (2.0 - 4.0 * p)


def angles(count):
    positions = np.arange(count)
    product = positions[:, None] * positions[None, :] % count
    angle = product * (2.0 * np.pi / count)
    return (np.cos(angle), np.sin(angle))


def complex_table(count, inverse):
    cosine, sine = angles(count)
    if inverse:
        cosine, sine = (cosine / count, -sine / count)
    rows_real = np.stack([cosine, -sine], 1)
    rows_imag = np.stack([sine, cosine], 1)
    return np.stack([rows_real, rows_imag], 0)


def halves(table):
    table = np.asarray(table, np.float32)
    high = np.asarray(table, BF16)
    low = np.asarray(table - high.astype(np.float32), BF16)
    return high, low


def split(value):
    high = value.astype(BF16)
    return high, (value - high.astype(F32)).astype(BF16)


def product(left, right, dims=(((1,), (0,)), ((), ()))):
    def one(a, b):
        return lax.dot_general(a, b, dims, preferred_element_type=F32)

    return one(left[0], right[0]) + (one(left[0], right[1]) + one(left[1], right[0]))


def wave(index, count, odd):
    signed = jnp.where(index < count // 2, index, index - count)
    if odd:
        signed = jnp.where(index == count // 2, 0, signed)
    return signed.astype(F32) * (2.0 * math.pi / count)


def middle_kernel(
    sizes, extra, base_ref, lines_ref, cos_h, cos_l, sin_h, sin_l, fwd_h, fwd_l, back_h, back_l, out_ref, spec, keep
):
    size_gy, size_gz, count_x = sizes
    local_z = lines_ref.shape[3]
    width = lines_ref.shape[4]
    count_z = local_z * size_gz
    count_y = spec.shape[2]
    step = pl.program_id(0)
    index_x = base_ref[0] + jnp.maximum(step - extra, 0)
    packed = index_x == 0
    top = jnp.logical_and(packed, step < extra)
    lane = lax.broadcasted_iota(jnp.int32, (count_z, size_gy * width), 1)
    is_real = (lane % width) < width // 2

    def plane():
        def forward(comp, carry):
            rows = []
            for y in range(size_gy):
                parts = [lines_ref[y * size_gz + z, 0, comp] for z in range(size_gz)]
                rows.append(jnp.concatenate(parts, 0))
            if extra:
                moved = [jnp.where(top, pltpu.roll(row, width // 2, 1), row) for row in rows]
                value = jnp.concatenate(moved, 1)
                value = jnp.where(jnp.logical_and(packed, jnp.logical_not(is_real)), 0.0, value)
            else:
                value = jnp.concatenate(rows, 1)
            value = product(split(value), (fwd_h[...], fwd_l[...]))
            real, imag = (split(value[:, :count_y]), split(value[:, count_y:]))
            cosine = (cos_h[...], cos_l[...])
            sine = (sin_h[...], sin_l[...])
            spec[comp] = product(cosine, real) + product(sine, imag)
            spec[3 + comp] = product(cosine, imag) - product(sine, real)
            return carry

        lax.fori_loop(0, 3, forward, 0)
        wave_x = wave(jnp.full((1, 1), index_x, jnp.int32), count_x, False)
        wave_x = jnp.where(top, math.pi, wave_x)
        curl_x = jnp.where(packed, 0.0, wave_x)
        tall = 64
        for first in range(0, count_z, tall):
            rows = pl.ds(first, tall)
            index_z = first + lax.broadcasted_iota(jnp.int32, (tall, 1), 0)
            index_y = lax.broadcasted_iota(jnp.int32, (1, count_y), 1)
            wave_z, wave_y = (wave(index_z, count_z, False), wave(index_y, count_y, False))
            curl_z, curl_y = (wave(index_z, count_z, True), wave(index_y, count_y, True))
            squared = wave_x * wave_x + wave_y * wave_y + wave_z * wave_z
            inverse = jnp.where(squared > 0, 1.0 / jnp.where(squared > 0, squared, 1.0), 0.0)
            inverse = inverse * (1.0 / count_z)
            for part, sign in ((3, -1.0), (0, 1.0)):
                scaled = inverse * sign
                s0, s1, s2 = [spec[part + comp, rows, :] * scaled for comp in range(3)]
                values = (curl_y * s2 - curl_z * s1, curl_z * s0 - curl_x * s2, curl_x * s1 - curl_y * s0)
                for comp in range(3):
                    spec[6 + (3 - part) + comp, rows, :] = values[comp]

        def backward(comp, carry):
            real, imag = (split(spec[6 + comp]), split(spec[9 + comp]))
            cosine = (cos_h[...], cos_l[...])
            sine = (sin_h[...], sin_l[...])
            value = jnp.concatenate(
                [
                    product(cosine, real) - product(sine, imag),
                    product(cosine, imag) + product(sine, real),
                ],
                1,
            )
            value = product(split(value), (back_h[...], back_l[...]))
            if extra:
                for y in range(size_gy):
                    cut = value[:, y * width : (y + 1) * width]

                    @pl.when(top)
                    def _():
                        keep[comp, :, y * width : (y + 1) * width] = pltpu.roll(cut, width // 2, 1)

                saved = keep[comp]
                merge = jnp.logical_and(packed, jnp.logical_not(is_real))
                value = jnp.where(merge, saved, value)
            for y in range(size_gy):
                for z in range(size_gz):
                    out_ref[y * size_gz + z, 0, comp] = value[
                        z * local_z : (z + 1) * local_z, y * width : (y + 1) * width
                    ]
            return carry

        lax.fori_loop(0, 3, backward, 0)

    if extra:
        pl.when(jnp.logical_or(step >= extra, packed))(plane)
    else:
        plane()


def middle(lines, base, tables, sizes, extra):
    size_gy, size_gz, count_x = sizes
    owners, share, _, local_z, width = lines.shape
    count_z = local_z * size_gz
    count_y = size_gy * width // 2
    shape = (owners, 1, 3, local_z, width)

    def at(step, base_ref):
        return (0, jnp.maximum(step - extra, 0), 0, 0, 0)

    def whole(table):
        return pl.BlockSpec(table.shape, lambda step, base_ref: (0, 0))

    flops = (share + extra) * 3 * 4 * 2 * 3 * count_z * (2 * count_y) ** 2
    return pl.pallas_call(
        functools.partial(middle_kernel, sizes, extra),
        grid_spec=pltpu.PrefetchScalarGridSpec(
            num_scalar_prefetch=1,
            grid=(share + extra,),
            in_specs=[pl.BlockSpec(shape, at)] + [whole(t) for t in tables],
            out_specs=pl.BlockSpec(shape, at),
            scratch_shapes=[
                pltpu.VMEM((12, count_z, count_y), F32),
                pltpu.VMEM((3, count_z, 2 * count_y) if extra else (1, 8, 128), F32),
            ],
        ),
        out_shape=jax.ShapeDtypeStruct(lines.shape, F32),
        compiler_params=pltpu.CompilerParams(
            dimension_semantics=("arbitrary",), vmem_limit_bytes=VMEM_BYTES
        ),
        cost_estimate=pl.CostEstimate(flops=flops, bytes_accessed=lines.size * 8, transcendentals=0),
        name="middle",
    )(base, lines, *tables)


def speed_kernel(chunks, tall, drift_ref, *refs):
    lines = refs[:chunks]
    table_h, table_l, thin_h, thin_l, out_ref, thin_ref = refs[chunks:]
    width = lines[0].shape[3]
    half = width // 2
    comp = pl.program_id(0)
    rows = []
    for z in range(tall):
        value = jnp.concatenate([ref[:, 0, z, :] for ref in lines], 0)
        turned = value.T
        rows.append(jnp.concatenate([turned[:half], turned[half:]], 1))
    left = split(jnp.concatenate(rows, 0))
    value = product(left, (table_h[...], table_l[...])) + drift_ref[comp]
    out_ref[0] = value.reshape(tall, half, value.shape[1])
    contract = (((1,), (1,)), ((), ()))
    thin_ref[0] = product((thin_h[...], thin_l[...]), left, contract) + drift_ref[comp]


def speed(parts, drift, tables):
    chunks = len(parts)
    depth, _, local_z, width = parts[0].shape
    count_x = tables[0].shape[1]
    half = width // 2
    tall = 8
    return pl.pallas_call(
        functools.partial(speed_kernel, chunks, tall),
        grid_spec=pltpu.PrefetchScalarGridSpec(
            num_scalar_prefetch=1,
            grid=(3, local_z // tall),
            in_specs=[pl.BlockSpec((depth, 1, tall, width), lambda c, z, d: (0, c, z, 0))] * chunks
            + [pl.BlockSpec(t.shape, lambda c, z, d: (0, 0)) for t in tables],
            out_specs=[
                pl.BlockSpec((1, tall, half, count_x), lambda c, z, d: (c, z, 0, 0)),
                pl.BlockSpec((1, 8, tall * half), lambda c, z, d: (c, 0, z)),
            ],
        ),
        out_shape=[
            jax.ShapeDtypeStruct((3, local_z, half, count_x), F32),
            jax.ShapeDtypeStruct((3, 8, local_z * half), F32),
        ],
        compiler_params=pltpu.CompilerParams(
            dimension_semantics=("arbitrary", "arbitrary"), vmem_limit_bytes=VMEM_BYTES
        ),
        cost_estimate=pl.CostEstimate(
            flops=6 * 3 * local_z * half * count_x * 2 * count_x // 2,
            bytes_accessed=24 * local_z * half * count_x,
            transcendentals=0,
        ),
        name="speed",
    )(drift, *parts, *tables)


def remesh_kernel(
    wake_ref, v_ref, vl_ref, vh_ref, vzl_ref, vzh_ref, f_ref, fl_ref, fh_ref, fzl_ref, fzh_ref,
    ghost_ref, pick_ref, out_ref, speeds, field, moved, ghosts, total,
):
    local_y, count_x = v_ref.shape[2:]
    step = pl.program_id(0)
    local_z = pl.num_programs(0) - 6
    wake = wake_ref[0] == 1
    edge = 8
    here = step % 3

    @pl.when(step == 0)
    def _():
        speeds[...] = jnp.zeros_like(speeds)
        field[...] = jnp.zeros_like(field)
        total[...] = jnp.zeros_like(total)

    @pl.when(step < 3)
    def _():
        speeds[here, :, edge - 4 : edge + local_y + 4] = vzl_ref[:, 0]

    @pl.when(step >= local_z + 3)
    def _():
        speeds[here, :, edge - 4 : edge + local_y + 4] = vzh_ref[:, 0]

    @pl.when(jnp.logical_and(step >= 3, step < local_z + 3))
    def _():
        speeds[here, :, edge - 4 : edge] = vl_ref[:, 0]
        speeds[here, :, edge : edge + local_y] = v_ref[:, 0]
        speeds[here, :, edge + local_y : edge + local_y + 4] = vh_ref[:, 0]

    @pl.when(step < 4)
    def _():
        field[:, edge - 2 : edge + local_y + 2] = fzl_ref[:, 0]

    @pl.when(step >= local_z + 4)
    def _():
        field[:, edge - 2 : edge + local_y + 2] = fzh_ref[:, 0]

    @pl.when(jnp.logical_and(step >= 4, step < local_z + 4))
    def _():
        field[:, edge - 2 : edge] = fl_ref[:, 0]
        field[:, edge : edge + local_y] = f_ref[:, 0]
        field[:, edge + local_y : edge + local_y + 2] = fh_ref[:, 0]

    @pl.when(step >= 2)
    def _():
        now, before = ((step + 2) % 3, (step + 1) % 3)
        ghosts[...] = lax.dot_general(
            ghost_ref[0], pick_ref[...], (((0,), (0,)), ((), ())),
            preferred_element_type=F32, precision=lax.Precision.HIGHEST,
        )
        lane = lax.broadcasted_iota(jnp.int32, (8, count_x), 1)
        first = jnp.logical_and(lane == 0, wake)
        last = jnp.logical_and(lane == count_x - 1, wake)
        cut = {
            offset: jnp.logical_and(lane >= count_x - offset if offset > 0 else lane < -offset, wake)
            for offset in (-2, -1, 1, 2)
        }
        total_rows = local_y + 2 * edge

        def wide(value):
            return jnp.concatenate([value, jnp.zeros((8, count_x - 128), F32)], 1)

        for row in range(0, total_rows, 8):
            rows = slice(row, row + 8)
            vel = [speeds[now, comp, rows] for comp in range(3)]
            vor = [field[comp, rows] * 0.125 for comp in range(3)]
            strength = []
            for comp in range(3):
                v = vel[comp]
                left = pltpu.roll(v, 1, 1)
                ghost = wide(ghosts[rows, comp * 128 : (comp + 1) * 128])
                left = jnp.where(first, ghost, left)
                right = jnp.where(last, v, pltpu.roll(v, count_x - 1, 1))
                if row == 0:
                    down = pltpu.roll(v, 1, 0)
                else:
                    down = speeds[now, comp, row - 1 : row + 7]
                if row == total_rows - 8:
                    up = pltpu.roll(v, 7, 0)
                else:
                    up = speeds[now, comp, row + 1 : row + 9]
                away = speeds[here, comp, rows] - speeds[before, comp, rows]
                pulled = vor[0] * (right - left) + vor[1] * (up - down) + vor[2] * away
                strength.append(vor[comp] + (0.5 * TIME_STEP) * pulled)
            shift = TIME_STEP * vel[0]
            sums = [strength[comp] * double_weight(-shift) for comp in range(3)]
            for offset in (-2, -1, 1, 2):
                weight = jnp.where(cut[offset], 0.0, double_weight(offset - shift))
                for comp in range(3):
                    sums[comp] += pltpu.roll(strength[comp] * weight, offset % count_x, 1)
            for comp in range(3):
                extra = ghosts[rows, (3 + comp) * 128 : (4 + comp) * 128]
                moved[comp, rows] = sums[comp] + wide(extra)
        for row in range(edge, edge + local_y, 8):
            lateral = [0.0, 0.0, 0.0]
            for offset in range(-2, 3):
                rows = slice(row - offset, row - offset + 8)
                weight = double_weight(offset - TIME_STEP * speeds[now, 1, rows])
                for comp in range(3):
                    lateral[comp] += moved[comp, rows] * weight
            shift = TIME_STEP * speeds[now, 2, row : row + 8]
            rows = slice(row - edge, row - edge + 8)
            for offset in range(-2, 3):
                weight = double_weight(offset - shift)
                slot = (step + 5 + offset) % 5
                for comp in range(3):
                    term = lateral[comp] * weight
                    if offset == -2:
                        out_ref[comp, 0, rows] = total[slot, comp, rows] + term
                    elif offset == 2:
                        total[slot, comp, rows] = term
                    else:
                        total[slot, comp, rows] += term


def remesh(wake, v, v_rims, f, f_rims, ghost, pick):
    _, local_z, local_y, count_x = v.shape
    steps = local_z + 6
    tall = local_y + 16

    def plane(rows, delay, limit):
        return pl.BlockSpec(
            (3, 1, rows, count_x), lambda i, w: (0, jnp.clip(i - delay, 0, limit - 1), 0, 0)
        )

    in_specs = [
        plane(local_y, 3, local_z),
        plane(4, 3, local_z),
        plane(4, 3, local_z),
        plane(local_y + 8, 0, 3),
        plane(local_y + 8, local_z + 3, 3),
        plane(local_y, 4, local_z),
        plane(2, 4, local_z),
        plane(2, 4, local_z),
        plane(local_y + 4, 2, 2),
        plane(local_y + 4, local_z + 4, 2),
        pl.BlockSpec((1, COLUMNS, tall), lambda i, w: (jnp.clip(i - 2, 0, local_z + 3), 0, 0)),
        pl.BlockSpec(pick.shape, lambda i, w: (0, 0)),
    ]
    return pl.pallas_call(
        remesh_kernel,
        grid_spec=pltpu.PrefetchScalarGridSpec(
            num_scalar_prefetch=1,
            grid=(steps,),
            in_specs=in_specs,
            out_specs=pl.BlockSpec(
                (3, 1, local_y, count_x), lambda i, w: (0, jnp.clip(i - 6, 0, local_z - 1), 0, 0)
            ),
            scratch_shapes=[
                pltpu.VMEM((3, 3, tall, count_x), F32),
                pltpu.VMEM((3, tall, count_x), F32),
                pltpu.VMEM((3, tall, count_x), F32),
                pltpu.VMEM((tall, 6 * 128), F32),
                pltpu.VMEM((5, 3, local_y, count_x), F32),
            ],
        ),
        out_shape=jax.ShapeDtypeStruct(v.shape, F32),
        compiler_params=pltpu.CompilerParams(
            dimension_semantics=("arbitrary",), vmem_limit_bytes=VMEM_BYTES
        ),
        cost_estimate=pl.CostEstimate(flops=v.size * 150, bytes_accessed=v.size * 12, transcendentals=0),
        name="remesh",
    )(wake, v, *v_rims, f, *f_rims, ghost, pick)


def all_rims(cells, rows, planes):
    low, high = rims(cells, "gy", 2, rows)
    local_z = cells.shape[1]
    ends = []
    for part in (slice(local_z - planes, local_z), slice(0, planes)):
        ends.append(jnp.concatenate([low[:, part], cells[:, part], high[:, part]], 2))
    count = lax.axis_size("gz")
    z_low = lax.ppermute(ends[0], "gz", [(i, (i + 1) % count) for i in range(count)])
    z_high = lax.ppermute(ends[1], "gz", [((i + 1) % count, i) for i in range(count)])
    return low, high, z_low, z_high


def ghost_columns(field_planes, thin):
    inner = thin[:, :, 1:-1, 1:-1]
    grad_z = (thin[:, 1:3, 2:, 1:-1] - thin[:, 1:3, :-2, 1:-1]) * 0.5
    grad_y = (thin[:, 1:3, 1:-1, 2:] - thin[:, 1:3, 1:-1, :-2]) * 0.5
    grad_x = (inner[:, 2:4] - inner[:, 0:2]) * 0.5
    pulled = field_planes[0:1] * grad_x + field_planes[1:2] * grad_y + field_planes[2:3] * grad_z
    strength = field_planes + TIME_STEP * pulled
    shift = TIME_STEP * inner[0, 1:3]
    zero = strength[:, 0] * kernel_weight(2.0 - shift[0]) + strength[:, 1] * kernel_weight(1.0 - shift[1])
    one = strength[:, 1] * kernel_weight(2.0 - shift[1])
    columns = jnp.concatenate([inner[:, 2], zero, one], 0)
    columns = jnp.pad(columns, ((0, COLUMNS - columns.shape[0]), (0, 0), (6, 6)))
    return columns.transpose(1, 0, 2)


def body(vorticity, wind):
    field = vorticity[0]
    drift = wind[0]
    count_x = field.shape[3]
    half_x = count_x // 2
    size_gy = lax.axis_size("gy")
    size_gz = lax.axis_size("gz")
    owners = size_gy * size_gz
    local_z, local_y = field.shape[1:3]
    count_y = local_y * size_gy
    count_z = local_z * size_gz
    share = half_x // owners
    chunks = math.gcd(share, 4)
    part = share // chunks
    sizes = (size_gy, size_gz, count_x)
    wake = lax.axis_index("grp").astype(jnp.int32).reshape(1)
    owner = lax.axis_index("gy") * size_gz + lax.axis_index("gz")

    cosine_x, sine_x = angles(count_x)
    alternate = 1.0 - 2.0 * (np.arange(count_x) % 2)
    forward_cos = cosine_x[:, :half_x]
    forward_sin = np.concatenate([alternate[:, None], -sine_x[:, 1:half_x]], 1)
    back_cos = np.concatenate([cosine_x[:1], 2.0 * cosine_x[1:half_x]], 0) / count_x
    back_sin = np.concatenate([-alternate[None, :], 2.0 * sine_x[1:half_x]], 0) / -count_x

    table_y = complex_table(count_y, False)
    table_y = table_y.reshape(2, size_gy, local_y, 2 * count_y)
    table_y = table_y.transpose(1, 0, 2, 3).reshape(2 * count_y, 2 * count_y)
    back_y = complex_table(count_y, True)
    back_y = back_y.reshape(2 * count_y, 2, size_gy, local_y)
    back_y = back_y.transpose(0, 2, 1, 3).reshape(2 * count_y, 2 * count_y)
    cosine_z, sine_z = angles(count_z)
    tables = [jnp.asarray(h) for t in (cosine_z, sine_z, table_y, back_y) for h in halves(t)]

    def dot(letters, values, table):
        return jnp.einsum(letters, values, jnp.asarray(table, F32), precision=HIGH)

    pieces = []
    for chunk in range(chunks):
        def pick(table):
            return table.reshape(count_x, owners, chunks, part)[:, :, chunk].reshape(count_x, -1)

        lines = jnp.concatenate(
            [
                dot("czyx,xk->kczy", field, pick(forward_cos)),
                dot("czyx,xk->kczy", field, pick(forward_sin)),
            ],
            3,
        )
        pieces.append(lax.all_to_all(lines, ("gy", "gz"), split_axis=0, concat_axis=0, tiled=True))

    field_rims = all_rims(field, 2, 2)
    field_planes = rimmed(
        field[..., count_x - 2 :].transpose(0, 3, 1, 2), (("gy", 3), ("gz", 2)), 2
    )

    parts = []
    for chunk in range(chunks):
        base = (owner * share + chunk * part).astype(jnp.int32).reshape(1)
        lines = pieces[chunk].reshape(owners, part, 3, local_z, 2 * local_y)
        lines = middle(lines, base, tables, sizes, 1 if chunk == 0 else 0)
        lines = lines.reshape(owners * part, 3, local_z, 2 * local_y)
        parts.append(lax.all_to_all(lines, ("gy", "gz"), split_axis=0, concat_axis=0, tiled=True))

    def turned(table):
        return table.reshape(owners, chunks, part, -1).transpose(1, 0, 2, 3).reshape(half_x, -1)

    back = np.concatenate([turned(back_cos), turned(back_sin)], 0)
    thin = np.zeros((8, count_x))
    thin[:4] = back[:, [count_x - 3, count_x - 2, count_x - 1, 0]].T
    speed_tables = [jnp.asarray(h) for t in (back, thin) for h in halves(t)]
    velocity, thin = speed(parts, drift, speed_tables)

    velocity_rims = all_rims(velocity, 4, 3)
    thin = thin.reshape(3, 8, local_z, local_y)[:, :4]
    thin = rimmed(thin, (("gy", 3), ("gz", 2)), 3)
    ghost = shifted(ghost_columns(field_planes, thin), "grp", 1)
    choose = np.zeros((COLUMNS, 6, 128), np.float32)
    for comp in range(3):
        choose[comp, comp, 0] = 1.0
        choose[3 + comp, 3 + comp, 0] = 0.25
        choose[6 + comp, 3 + comp, 1] = 0.25
    choose = jnp.asarray(choose.reshape(COLUMNS, 6 * 128))
    result = remesh(wake, velocity, velocity_rims, field, field_rims, ghost, choose)
    return (result[None], velocity[None])


def solution(mesh):
    return jax.shard_map(
        body,
        mesh=mesh,
        in_specs=(P("grp", None, "gz", "gy", None), P("grp", None)),
        out_specs=(P("grp", None, "gz", "gy", None), P("grp", None, "gz", "gy", None)),
        check_vma=False,
    )
```

time: 1240 us -> 973 us (0.78)
  other arithmetic: 339 us -> 13.7 us
  Pallas kernels: 0 us -> 242 us
  waiting for transfers between devices: 456 us -> 287 us
  matrix products: 223 us -> 90 us
  starting transfers between devices: 63 us -> 149 us
  local copies, waits for them, and re-layouts: 148 us -> 182 us
    pallas_call x0 -> x6, Pallas kernels: none -> 242 us  [the longest x1 118 us: remesh(): pl.pallas_call(remesh_kernel, grid_spec=pltpu.PrefetchScalarGridSpec(num_...]
    ppermute x26 -> x16, waiting for transfers between devices: 189 us -> 53.1 us  [the longest x6 41.7 us: rims(): lax.ppermute(head, axis, [((i + 1) % count, i) for i in range(count)])]
    dot_general x51 -> x8, matrix products: 223 us -> 90 us  [dot(): return jnp.einsum(letters, values, jnp.asarray(table, F32), precision=HIGH)]
    add x6 -> x2, other arithmetic: 124 us -> 2.19 us  [the longest x1 2.1 us: ghost_columns(): strength = field_planes + TIME_STEP * pulled]
    all_to_all x6 -> x8, starting transfers between devices: 31.6 us -> 123 us  [body(): lax.all_to_all(lines, ('gy', 'gz'), split_axis=0, concat_axis=0, tiled=True)]
    concatenate x17 -> x10, other arithmetic: 61 us -> 7.53 us  [the longest x4 3.51 us: body(): jnp.concatenate([dot('czyx,xk->kczy', field, pick(forward_cos)), dot('czy...]
    broadcast_in_dim x2 -> x0, other arithmetic: 38.8 us -> none  [body(): return (result[None], velocity[None])]
    mul x9 -> x2, other arithmetic: 39 us -> 0.68 us  [the longest x1 0.5 us: ghost_columns(): shift = TIME_STEP * inner[0, 1:3]]
  transfers between devices with their start and end apart: 34 -> 25, of which waited for: 23 -> 13; matrix products, arithmetic and copies ran while one was open for 24% -> 21% of each run, Pallas kernels for 0% -> 13%
where the time goes in v1:
time: 973 us; the launch traced here: 966 us
  waiting for transfers between devices  287 us (29%)
  Pallas kernels  242 us (25%)
  local copies, waits for them, and re-layouts  182 us (19%)
  starting transfers between devices  149 us (15%)
  matrix products  90 us (9%)
  other arithmetic  13.7 us (1%)
    all_to_all x8, waiting for transfers between devices, body(): lax.all_to_all(lines, ('gy', 'gz'), split_axis=0, concat_axis=0, tiled=True)  230 us
    all_to_all x8, starting transfers between devices, body(): lax.all_to_all(lines, ('gy', 'gz'), split_axis=0, concat_axis=0, tiled=True)  123 us
    pallas_call x1, Pallas kernels, remesh(): pl.pallas_call(remesh_kernel, grid_spec=pltpu.PrefetchScalarGridSpec(num_...  118 us
    pallas_call x4, Pallas kernels, middle(): pl.pallas_call(functools.partial(middle_kernel, sizes, extra), grid_spec=...  96.3 us
    dot_general x8, matrix products, dot(): return jnp.einsum(letters, values, jnp.asarray(table, F32), precision=HIGH)  90 us
    slice x3, local copies, waits for them, and re-layouts, rims(): head = lax.slice_in_dim(cells, 0, width, axis=dim)  69.9 us
    ppermute x6, waiting for transfers between devices, rims(): lax.ppermute(head, axis, [((i + 1) % count, i) for i in range(count)])  41.7 us
    unnamed x50, local copies, waits for them, and re-layouts  35.6 us
  transfers between devices with their start and end apart: 25, of which 13 were waited for; matrix products, arithmetic and copies ran while one was open for 21% of the time, Pallas kernels for 13%

profile of v1, /device:TPU:0, one launch (start us, length us, event | category | flops | bytes accessed | tf_op | source)
XLA Modules:
  0.0 965.7 jit_solution(4741752531822686494)
XLA Ops:
  0.6 26.3 %copy.64 = f32[1,3,64,64,256]{3,1,2,4,0:T(4,128)} copy(f32[1,3,64,64,256]{4,3,2,1,0:T(8,128)} %param.23) | data formatting | bytes 25165824 | tf_op args[0]
  27.0 26.4 %copy.65.f_ref = f32[3,64,64,256]{3,2,1,0:T(8,128)} copy(f32[3,64,64,256]{2,0,1,3:T(4,128)} %bitcast.115) | data formatting | bytes 25165824 | tf_op jit(solution)/shard_map/squeeze | solution.py:474
  53.3 11.9 %fusion.35 = f32[32,3,64,64]{3,0,2,1:T(8,128)S(1)} fusion(f32[256,32,1,1]{0,1,3,2:T(8,128)S(1)} %copy-done.15, f32[3,64,64,256]{3,2,1,0:T(8,128)} %copy.65.f_ref), kind=kOutput, calls=%fused_computation.95 | convolution fusion | flops 603979776 | bytes 14188544 | tf_op jit(solution)/shard_map/czyx,xk->kczy/dot_general | solution.py:508
  86.3 11.5 %fusion.37 = f32[32,3,64,64]{3,0,2,1:T(8,128)S(1)} fusion(f32[256,32,1,1]{0,1,3,2:T(8,128)S(1)} %copy-done.14, f32[3,64,64,256]{3,2,1,0:T(8,128)} %copy.65.f_ref), kind=kOutput, calls=%fused_computation.97 | convolution fusion | flops 603979776 | bytes 14188544 | tf_op jit(solution)/shard_map/czyx,xk->kczy/dot_general | solution.py:508
  97.9 11.5 %fusion.36 = f32[32,3,64,64]{3,0,2,1:T(8,128)S(1)} fusion(f32[256,32,1,1]{0,1,3,2:T(8,128)S(1)} %copy-done.13, f32[3,64,64,256]{3,2,1,0:T(8,128)} %copy.65.f_ref), kind=kOutput, calls=%fused_computation.96 | convolution fusion | flops 603979776 | bytes 14188544 | tf_op jit(solution)/shard_map/czyx,xk->kczy/dot_general | solution.py:508
  113.8 31.7 %all-to-all-done = f32[32,3,64,128]{3,2,1,0:T(8,128)S(1)} async-done(((f32[32,3,64,128]{3,2,1,0:T(8,128)}), f32[32,3,64,128]{3,2,1,0:T(8,128)S(1)}, u32[]{:S(2)}, u32[]{:S(2)}) %all-to-all-start) | async-done | bytes 3145760 | tf_op jit(solution)/shard_map/all_to_all | solution.py:522
  147.2 15.9 %all-to-all-start.2 = ((f32[32,3,64,128]{3,2,1,0:T(8,128)}), f32[32,3,64,128]{3,2,1,0:T(8,128)}, u32[]{:S(2)}, u32[]{:S(2)}) async-start(f32[32,3,64,128]{3,2,1,0:T(8,128)} %copy.70), calls=%async_computation.2 | async-start | bytes 6291456 | tf_op jit(solution)/shard_map/all_to_all | solution.py:522
  174.7 11.5 %fusion.38 = f32[32,3,64,64]{3,0,2,1:T(8,128)S(1)} fusion(f32[256,32,1,1]{0,1,3,2:T(8,128)S(1)} %copy-done.11, f32[3,64,64,256]{3,2,1,0:T(8,128)} %copy.65.f_ref), kind=kOutput, calls=%fused_computation.98 | convolution fusion | flops 603979776 | bytes 14188544 | tf_op jit(solution)/shard_map/czyx,xk->kczy/dot_general | solution.py:508
  190.7 31.7 %all-to-all-done.2 = f32[32,3,64,128]{3,2,1,0:T(8,128)} async-done(((f32[32,3,64,128]{3,2,1,0:T(8,128)}), f32[32,3,64,128]{3,2,1,0:T(8,128)}, u32[]{:S(2)}, u32[]{:S(2)}) %all-to-all-start.2) | async-done | bytes 3145760 | tf_op jit(solution)/shard_map/all_to_all | solution.py:522
  222.4 15.6 %all-to-all-start.4 = ((f32[32,3,64,128]{3,2,1,0:T(8,128)}), f32[32,3,64,128]{3,2,1,0:T(8,128)S(1)}, u32[]{:S(2)}, u32[]{:S(2)}) async-start(f32[32,3,64,128]{3,2,1,0:T(8,128)} %copy.73), calls=%async_computation.4 | async-start | bytes 6291456 | tf_op jit(solution)/shard_map/all_to_all | solution.py:522
  238.0 11.5 %fusion.41 = f32[32,3,64,64]{3,0,2,1:T(8,128)S(1)} fusion(f32[256,32,1,1]{0,1,3,2:T(8,128)S(1)} %copy-done.10, f32[3,64,64,256]{3,2,1,0:T(8,128)} %copy.65.f_ref), kind=kOutput, calls=%fused_computation.101 | convolution fusion | flops 603979776 | bytes 14188544 | tf_op jit(solution)/shard_map/czyx,xk->kczy/dot_general | solution.py:508
  249.6 11.5 %fusion.40 = f32[32,3,64,64]{3,0,2,1:T(8,128)S(1)} fusion(f32[256,32,1,1]{0,1,3,2:T(8,128)S(1)} %copy-done.9, f32[3,64,64,256]{3,2,1,0:T(8,128)} %copy.65.f_ref), kind=kOutput, calls=%fused_computation.100 | convolution fusion | flops 603979776 | bytes 14188544 | tf_op jit(solution)/shard_map/czyx,xk->kczy/dot_general | solution.py:508
  265.5 31.8 %all-to-all-done.4 = f32[32,3,64,128]{3,2,1,0:T(8,128)S(1)} async-done(((f32[32,3,64,128]{3,2,1,0:T(8,128)}), f32[32,3,64,128]{3,2,1,0:T(8,128)S(1)}, u32[]{:S(2)}, u32[]{:S(2)}) %all-to-all-start.4) | async-done | bytes 3145760 | tf_op jit(solution)/shard_map/all_to_all | solution.py:522
  299.0 15.6 %all-to-all-start.6 = ((f32[32,3,64,128]{3,2,1,0:T(8,128)}), f32[32,3,64,128]{3,2,1,0:T(8,128)S(1)}, u32[]{:S(2)}, u32[]{:S(2)}) async-start(f32[32,3,64,128]{3,2,1,0:T(8,128)} %copy.76), calls=%async_computation.6 | async-start | bytes 6291456 | tf_op jit(solution)/shard_map/all_to_all | solution.py:522
  314.6 31.8 %middle.4 = f32[16,2,3,64,128]{4,3,2,1,0:T(8,128)} custom-call(s32[1]{0:T(128)} %bitcast.2.base_ref, f32[16,2,3,64,128]{4,3,2,1,0:T(8,128)} %bitcast.123, bf16[256,256]{1,0:T(8,128)(2,1)} %constant.81.clone.cos_h, bf16[256,256]{1,0:T(8,128)(2,1)} %constant.82.clone.cos_l, bf16[256,256]{1,0:T(8,128)(2,1)} %constant.83.clone.sin_h, ...), custom_call_target="tpu_custom_call" | custom-call | flops 14495514624 | bytes 6291456 | tf_op jit(solution)/shard_map/middle/pallas_call | solution.py:206
  346.4 27.4 %all-to-all-done.6 = f32[32,3,64,128]{3,2,1,0:T(8,128)S(1)} async-done(((f32[32,3,64,128]{3,2,1,0:T(8,128)}), f32[32,3,64,128]{3,2,1,0:T(8,128)S(1)}, u32[]{:S(2)}, u32[]{:S(2)}) %all-to-all-start.6) | async-done | bytes 3145760 | tf_op jit(solution)/shard_map/all_to_all | solution.py:522
  375.4 15.4 %all-to-all-start.1 = ((f32[32,3,64,128]{3,2,1,0:T(8,128)}), f32[32,3,64,128]{3,2,1,0:T(8,128)S(1)}, u32[]{:S(2)}, u32[]{:S(2)}) async-start(f32[32,3,64,128]{3,2,1,0:T(8,128)} %bitcast.127), calls=%async_computation.1 | async-start | bytes 6291456 | tf_op jit(solution)/shard_map/all_to_all | solution.py:535
  390.9 21.5 %middle.5 = f32[16,2,3,64,128]{4,3,2,1,0:T(8,128)} custom-call(s32[1]{0:T(128)} %bitcast.10.base_ref, f32[16,2,3,64,128]{4,3,2,1,0:T(8,128)} %bitcast.15.lines_ref, bf16[256,256]{1,0:T(8,128)(2,1)} %constant.81.clone.cos_h, bf16[256,256]{1,0:T(8,128)(2,1)} %constant.82.clone.cos_l, bf16[256,256]{1,0:T(8,128)(2,1)} %constant.83.clone.sin_h, ...), custom_call_target="tpu_custom_call" | custom-call | flops 9663676416 | bytes 6291456 | tf_op jit(solution)/shard_map/middle/pallas_call | solution.py:206
  412.4 37.7 %all-to-all-done.1.refs_0_ = f32[32,3,64,128]{3,2,1,0:T(8,128)S(1)} async-done(((f32[32,3,64,128]{3,2,1,0:T(8,128)}), f32[32,3,64,128]{3,2,1,0:T(8,128)S(1)}, u32[]{:S(2)}, u32[]{:S(2)}) %all-to-all-start.1) | async-done | bytes 3145760 | tf_op jit(solution)/shard_map/all_to_all | solution.py:535
  451.8 15.5 %all-to-all-start.3 = ((f32[32,3,64,128]{3,2,1,0:T(8,128)}), f32[32,3,64,128]{3,2,1,0:T(8,128)}, u32[]{:S(2)}, u32[]{:S(2)}) async-start(f32[32,3,64,128]{3,2,1,0:T(8,128)} %bitcast.126), calls=%async_computation.3 | async-start | bytes 6291456 | tf_op jit(solution)/shard_map/all_to_all | solution.py:535
  467.3 21.5 %middle.6 = f32[16,2,3,64,128]{4,3,2,1,0:T(8,128)} custom-call(s32[1]{0:T(128)} %bitcast.17.base_ref, f32[16,2,3,64,128]{4,3,2,1,0:T(8,128)} %bitcast.124, bf16[256,256]{1,0:T(8,128)(2,1)} %constant.81.clone.cos_h, bf16[256,256]{1,0:T(8,128)(2,1)} %constant.82.clone.cos_l, bf16[256,256]{1,0:T(8,128)(2,1)} %constant.83.clone.sin_h, ...), custom_call_target="tpu_custom_call" | custom-call | flops 9663676416 | bytes 6291456 | tf_op jit(solution)/shard_map/middle/pallas_call | solution.py:206
  488.8 37.8 %all-to-all-done.3.refs_1_ = f32[32,3,64,128]{3,2,1,0:T(8,128)} async-done(((f32[32,3,64,128]{3,2,1,0:T(8,128)}), f32[32,3,64,128]{3,2,1,0:T(8,128)}, u32[]{:S(2)}, u32[]{:S(2)}) %all-to-all-start.3) | async-done | bytes 3145760 | tf_op jit(solution)/shard_map/all_to_all | solution.py:535
  526.5 15.4 %all-to-all-start.5 = ((f32[32,3,64,128]{3,2,1,0:T(8,128)}), f32[32,3,64,128]{3,2,1,0:T(8,128)S(1)}, u32[]{:S(2)}, u32[]{:S(2)}) async-start(f32[32,3,64,128]{3,2,1,0:T(8,128)} %bitcast.125), calls=%async_computation.5 | async-start | bytes 6291456 | tf_op jit(solution)/shard_map/all_to_all | solution.py:535
  547.7 21.5 %middle.7 = f32[16,2,3,64,128]{4,3,2,1,0:T(8,128)} custom-call(s32[1]{0:T(128)} %bitcast.24.base_ref, f32[16,2,3,64,128]{4,3,2,1,0:T(8,128)} %bitcast.122, bf16[256,256]{1,0:T(8,128)(2,1)} %constant.81.clone.cos_h, bf16[256,256]{1,0:T(8,128)(2,1)} %constant.82.clone.cos_l, bf16[256,256]{1,0:T(8,128)(2,1)} %constant.83.clone.sin_h, ...), custom_call_target="tpu_custom_call" | custom-call | flops 9663676416 | bytes 6291456 | tf_op jit(solution)/shard_map/middle/pallas_call | solution.py:206
  569.2 32.0 %all-to-all-done.5.refs_2_ = f32[32,3,64,128]{3,2,1,0:T(8,128)S(1)} async-done(((f32[32,3,64,128]{3,2,1,0:T(8,128)}), f32[32,3,64,128]{3,2,1,0:T(8,128)S(1)}, u32[]{:S(2)}, u32[]{:S(2)}) %all-to-all-start.5) | async-done | bytes 3145760 | tf_op jit(solution)/shard_map/all_to_all | solution.py:535
  602.9 21.9 %all-to-all-start.7 = ((f32[32,3,64,128]{3,2,1,0:T(8,128)}), f32[32,3,64,128]{3,2,1,0:T(8,128)}, u32[]{:S(2)}, u32[]{:S(2)}) async-start(f32[32,3,64,128]{3,2,1,0:T(8,128)} %bitcast.121), calls=%async_computation.7 | async-start | bytes 6291456 | tf_op jit(solution)/shard_map/all_to_all | solution.py:535
  624.8 45.9 %fusion.25 = (f32[3,64,2,256]{2,0,1,3:T(4,128)}, f32[3,64,2,256]{2,0,1,3:T(4,128)}) fusion(f32[3,64,64,256]{2,0,1,3:T(4,128)} %bitcast.117), kind=kLoop, calls=%fused_computation.85 | loop fusion | bytes 1572864 | tf_op jit(solution)/shard_map/slice | solution.py:28
  670.7 21.9 %copy.77 = f32[3,64,2,256]{3,1,2,0:T(8,128)} copy(f32[3,64,2,256]{2,0,1,3:T(4,128)} %get-tuple-element.9) | data formatting | bytes 786432 | tf_op jit(solution)/shard_map/slice | solution.py:29
  694.6 21.9 %copy.78 = f32[3,64,2,256]{3,1,2,0:T(8,128)} copy(f32[3,64,2,256]{2,0,1,3:T(4,128)} %get-tuple-element.8) | data formatting | bytes 786432 | tf_op jit(solution)/shard_map/slice | solution.py:28
  731.2 27.2 %speed.1 = (f32[3,64,64,256]{3,2,1,0:T(8,128)}, f32[3,8,4096]{2,1,0:T(8,128)}) custom-call(f32[3]{0:T(128)} %bitcast.130, f32[32,3,64,128]{3,2,1,0:T(8,128)} %copy-done.1, f32[32,3,64,128]{3,2,1,0:T(8,128)} %all-to-all-done.3.refs_1_, f32[32,3,64,128]{3,2,1,0:T(8,128)} %copy-done.2, f32[32,3,64,128]{3,2,1,0:T(8,128)} %all-to-all-done.7.refs_3_, ...), custom_call_target="tpu_custom_call" | custom-call | flops 4831838208 | bytes 25165824 | tf_op jit(solution)/shard_map/speed/pallas_call | solution.py:251
  797.4 30.5 %collective-permute-done.1.vh_ref = f32[3,64,4,256]{3,2,1,0:T(4,128)S(1)} collective-permute-done((f32[3,64,4,256]{3,2,1,0:T(4,128)S(1)}, f32[3,64,4,256]{3,2,1,0:T(4,128)S(1)}, u32[]{:S(2)}, u32[]{:S(2)}) %collective-permute-start.1) | collective-permute-done | bytes 786464 | tf_op jit(solution)/shard_map/ppermute | solution.py:31
  846.9 118.3 %remesh.1 = f32[3,64,64,256]{3,2,1,0:T(8,128)} custom-call(s32[1]{0:T(128)} %bitcast.wake_ref, f32[3,64,64,256]{3,2,1,0:T(8,128)} %get-tuple-element.4.v_ref, f32[3,64,4,256]{3,2,1,0:T(4,128)} %copy-done.6, f32[3,64,4,256]{3,2,1,0:T(4,128)} %copy-done.7, f32[3,3,72,256]{3,2,1,0:T(8,128)} %collective-permute-done.2.vzl_ref, ...), custom_call_target="tpu_custom_call" | custom-call | flops 471859200 | bytes 37748736 | tf_op jit(solution)/shard_map/remesh/pallas_call | solution.py:420
  (127 shorter events, 134.2 us)
Async XLA Ops:
  27.0 26.4 %copy-start.15 = (f32[256,32,1,1]{0,1,3,2:T(8,128)S(1)}, f32[256,32,1,1]{0,1,3,2:T(8,128)}, u32[]{:S(2)}) copy-start(f32[256,32,1,1]{0,1,3,2:T(8,128)} %constant.107) | copy-start | bytes 98308
  53.3 11.9 %copy-start.16 = (f32[256,32,1,1]{0,1,3,2:T(8,128)S(1)}, f32[256,32,1,1]{0,1,3,2:T(8,128)}, u32[]{:S(2)}) copy-start(f32[256,32,1,1]{0,1,3,2:T(8,128)} %constant.106) | copy-start | bytes 98308
  78.5 67.0 %all-to-all-start = ((f32[32,3,64,128]{3,2,1,0:T(8,128)}), f32[32,3,64,128]{3,2,1,0:T(8,128)S(1)}, u32[]{:S(2)}, u32[]{:S(2)}) async-start(f32[32,3,64,128]{3,2,1,0:T(8,128)} %copy.67), calls=%async_computation | async-start | bytes 6291456 | tf_op jit(solution)/shard_map/all_to_all | solution.py:522
  113.8 49.3 %copy-start.12 = (f32[256,32,1,1]{0,1,3,2:T(8,128)S(1)}, f32[256,32,1,1]{0,1,3,2:T(8,128)}, u32[]{:S(2)}) copy-start(f32[256,32,1,1]{0,1,3,2:T(8,128)} %constant.111) | copy-start | bytes 98308
  147.2 75.2 %all-to-all-start.2 = ((f32[32,3,64,128]{3,2,1,0:T(8,128)}), f32[32,3,64,128]{3,2,1,0:T(8,128)}, u32[]{:S(2)}, u32[]{:S(2)}) async-start(f32[32,3,64,128]{3,2,1,0:T(8,128)} %copy.70), calls=%async_computation.2 | async-start | bytes 6291456 | tf_op jit(solution)/shard_map/all_to_all | solution.py:522
  190.7 47.3 %copy-start.10 = (f32[256,32,1,1]{0,1,3,2:T(8,128)S(1)}, f32[256,32,1,1]{0,1,3,2:T(8,128)}, u32[]{:S(2)}) copy-start(f32[256,32,1,1]{0,1,3,2:T(8,128)} %constant.113) | copy-start | bytes 98308
  222.4 74.8 %all-to-all-start.4 = ((f32[32,3,64,128]{3,2,1,0:T(8,128)}), f32[32,3,64,128]{3,2,1,0:T(8,128)S(1)}, u32[]{:S(2)}, u32[]{:S(2)}) async-start(f32[32,3,64,128]{3,2,1,0:T(8,128)} %copy.73), calls=%async_computation.4 | async-start | bytes 6291456 | tf_op jit(solution)/shard_map/all_to_all | solution.py:522
  299.0 74.9 %all-to-all-start.6 = ((f32[32,3,64,128]{3,2,1,0:T(8,128)}), f32[32,3,64,128]{3,2,1,0:T(8,128)S(1)}, u32[]{:S(2)}, u32[]{:S(2)}) async-start(f32[32,3,64,128]{3,2,1,0:T(8,128)} %copy.76), calls=%async_computation.6 | async-start | bytes 6291456 | tf_op jit(solution)/shard_map/all_to_all | solution.py:522
  375.4 74.7 %all-to-all-start.1 = ((f32[32,3,64,128]{3,2,1,0:T(8,128)}), f32[32,3,64,128]{3,2,1,0:T(8,128)S(1)}, u32[]{:S(2)}, u32[]{:S(2)}) async-start(f32[32,3,64,128]{3,2,1,0:T(8,128)} %bitcast.127), calls=%async_computation.1 | async-start | bytes 6291456 | tf_op jit(solution)/shard_map/all_to_all | solution.py:535
  451.8 74.8 %all-to-all-start.3 = ((f32[32,3,64,128]{3,2,1,0:T(8,128)}), f32[32,3,64,128]{3,2,1,0:T(8,128)}, u32[]{:S(2)}, u32[]{:S(2)}) async-start(f32[32,3,64,128]{3,2,1,0:T(8,128)} %bitcast.126), calls=%async_computation.3 | async-start | bytes 6291456 | tf_op jit(solution)/shard_map/all_to_all | solution.py:535
  526.5 74.7 %all-to-all-start.5 = ((f32[32,3,64,128]{3,2,1,0:T(8,128)}), f32[32,3,64,128]{3,2,1,0:T(8,128)S(1)}, u32[]{:S(2)}, u32[]{:S(2)}) async-start(f32[32,3,64,128]{3,2,1,0:T(8,128)} %bitcast.125), calls=%async_computation.5 | async-start | bytes 6291456 | tf_op jit(solution)/shard_map/all_to_all | solution.py:535
  543.9 174.3 %collective-permute-start.13 = (f32[3,2,64,2]{3,0,2,1:T(4,128)}, f32[3,2,64,2]{3,0,2,1:T(4,128)}, u32[]{:S(2)}, u32[]{:S(2)}) collective-permute-start(f32[3,2,64,2]{3,0,2,1:T(4,128)} %get-tuple-element.34), channel_id=1, source_target_pairs={{4,0},{8,4},{12,8},{0,12},{5,1},{9,5},{13,9},{1,13},{6,2},{10,6},{... | collective-permute-start | bytes 9224 | tf_op jit(solution)/shard_map/ppermute | solution.py:31
  547.7 170.6 %collective-permute-start.12 = (f32[3,2,64,2]{3,0,2,1:T(4,128)}, f32[3,2,64,2]{3,0,2,1:T(4,128)}, u32[]{:S(2)}, u32[]{:S(2)}) collective-permute-start(f32[3,2,64,2]{3,0,2,1:T(4,128)} %get-tuple-element.33), channel_id=1, source_target_pairs={{0,4},{4,8},{8,12},{12,0},{1,5},{5,9},{9,13},{13,1},{2,6},{6,10},{... | collective-permute-start | bytes 9224 | tf_op jit(solution)/shard_map/ppermute | solution.py:30
  602.9 128.3 %all-to-all-start.7 = ((f32[32,3,64,128]{3,2,1,0:T(8,128)}), f32[32,3,64,128]{3,2,1,0:T(8,128)}, u32[]{:S(2)}, u32[]{:S(2)}) async-start(f32[32,3,64,128]{3,2,1,0:T(8,128)} %bitcast.121), calls=%async_computation.7 | async-start | bytes 6291456 | tf_op jit(solution)/shard_map/all_to_all | solution.py:535
  692.6 35.0 %collective-permute-start.4 = (f32[3,64,2,256]{3,1,2,0:T(8,128)}, f32[3,64,2,256]{3,1,2,0:T(8,128)S(1)}, u32[]{:S(2)}, u32[]{:S(2)}) collective-permute-start(f32[3,64,2,256]{3,1,2,0:T(8,128)} %copy.77), channel_id=1, source_target_pairs={{0,4},{4,8},{8,12},{12,0},{1,5},{5,9},{9,13},{13,1},{2,6},{6,10},{... | collective-permute-start | bytes 1179656 | tf_op jit(solution)/shard_map/ppermute | solution.py:30
  716.4 11.1 %collective-permute-start.5 = (f32[3,64,2,256]{3,1,2,0:T(8,128)}, f32[3,64,2,256]{3,1,2,0:T(8,128)S(1)}, u32[]{:S(2)}, u32[]{:S(2)}) collective-permute-start(f32[3,64,2,256]{3,1,2,0:T(8,128)} %copy.78), channel_id=1, source_target_pairs={{4,0},{8,4},{12,8},{0,12},{5,1},{9,5},{13,9},{1,13},{6,2},{10,6},{... | collective-permute-start | bytes 1179656 | tf_op jit(solution)/shard_map/ppermute | solution.py:31
  719.7 4.1 collective-permute-start.15
  720.9 3.3 collective-permute-start.14
  727.5 30.9 %copy-start.8 = (f32[3,64,2,256]{3,1,2,0:T(8,128)}, f32[3,64,2,256]{3,1,2,0:T(8,128)S(1)}, u32[]{:S(2)}) copy-start(f32[3,64,2,256]{3,1,2,0:T(8,128)S(1)} %collective-permute-done.5) | copy-start | bytes 1179652
  728.5 110.4 %collective-permute-start.6 = (f32[3,2,68,256]{3,1,2,0:T(2,128)}, f32[3,2,68,256]{3,1,2,0:T(2,128)}, u32[]{:S(2)}, u32[]{:S(2)}) collective-permute-start(f32[3,2,68,256]{3,1,2,0:T(2,128)} %pad_maximum_fusion.7), channel_id=1, source_target_pairs={{0,1},{1,2},{2,3},{3,0},{4,5},{5,6},{6,7},{7,4},{8,9},{9,10},{10,1... | collective-permute-start | bytes 1253384 | tf_op jit(solution)/shard_map/ppermute | solution.py:453
  729.4 111.3 %collective-permute-start.7 = (f32[3,2,68,256]{3,1,2,0:T(2,128)}, f32[3,2,68,256]{3,1,2,0:T(2,128)}, u32[]{:S(2)}, u32[]{:S(2)}) collective-permute-start(f32[3,2,68,256]{3,1,2,0:T(2,128)} %pad_maximum_fusion.8), channel_id=1, source_target_pairs={{1,0},{2,1},{3,2},{0,3},{5,4},{6,5},{7,6},{4,7},{9,8},{10,9},{11,1... | collective-permute-start | bytes 1253384 | tf_op jit(solution)/shard_map/ppermute | solution.py:454
  760.2 16.4 %collective-permute-start.9 = (f32[3,4,64,3]{3,0,2,1:T(4,128)S(1)}, f32[3,4,64,3]{3,0,2,1:T(4,128)S(1)}, u32[]{:S(2)}, u32[]{:S(2)}) collective-permute-start(f32[3,4,64,3]{3,0,2,1:T(4,128)S(1)} %copy.105), channel_id=1, source_target_pairs={{4,0},{8,4},{12,8},{0,12},{5,1},{9,5},{13,9},{1,13},{6,2},{10,6},{... | collective-permute-start | bytes 27656 | tf_op jit(solution)/shard_map/ppermute | solution.py:31
  764.5 23.1 %collective-permute-start.8 = (f32[3,4,64,3]{3,0,2,1:T(4,128)S(1)}, f32[3,4,64,3]{3,0,2,1:T(4,128)S(1)}, u32[]{:S(2)}, u32[]{:S(2)}) collective-permute-start(f32[3,4,64,3]{3,0,2,1:T(4,128)S(1)} %copy.103), channel_id=1, source_target_pairs={{0,4},{4,8},{8,12},{12,0},{1,5},{5,9},{9,13},{13,1},{2,6},{6,10},{... | collective-permute-start | bytes 27656 | tf_op jit(solution)/shard_map/ppermute | solution.py:30
  787.7 3.8 collective-permute-start.11
  787.8 5.7 collective-permute-start.10
  789.6 38.3 %collective-permute-start = (f32[3,64,4,256]{3,2,1,0:T(4,128)S(1)}, f32[3,64,4,256]{3,2,1,0:T(4,128)S(1)}, u32[]{:S(2)}, u32[]{:S(2)}) collective-permute-start(f32[3,64,4,256]{3,2,1,0:T(4,128)S(1)} %get-tuple-element.13), channel_id=1, source_target_pairs={{0,4},{4,8},{8,12},{12,0},{1,5},{5,9},{9,13},{13,1},{2,6},{6,10},{... | collective-permute-start | bytes 2359304 | tf_op jit(solution)/shard_map/ppermute | solution.py:30
  791.5 36.4 %collective-permute-start.1 = (f32[3,64,4,256]{3,2,1,0:T(4,128)S(1)}, f32[3,64,4,256]{3,2,1,0:T(4,128)S(1)}, u32[]{:S(2)}, u32[]{:S(2)}) collective-permute-start(f32[3,64,4,256]{3,2,1,0:T(4,128)S(1)} %get-tuple-element.12), channel_id=1, source_target_pairs={{4,0},{8,4},{12,8},{0,12},{5,1},{9,5},{13,9},{1,13},{6,2},{10,6},{... | collective-permute-start | bytes 2359304 | tf_op jit(solution)/shard_map/ppermute | solution.py:31
  827.9 12.8 %copy-start.7 = (f32[3,64,4,256]{3,2,1,0:T(4,128)}, f32[3,64,4,256]{3,2,1,0:T(4,128)S(1)}, u32[]{:S(2)}) copy-start(f32[3,64,4,256]{3,2,1,0:T(4,128)S(1)} %collective-permute-done.1.vh_ref) | copy-start | bytes 2359300
  827.9 12.8 %copy-start.6 = (f32[3,64,4,256]{3,2,1,0:T(4,128)}, f32[3,64,4,256]{3,2,1,0:T(4,128)S(1)}, u32[]{:S(2)}) copy-start(f32[3,64,4,256]{3,2,1,0:T(4,128)S(1)} %collective-permute-done.vl_ref) | copy-start | bytes 2359300
  828.0 18.9 %collective-permute-start.2 = (f32[3,3,72,256]{3,2,1,0:T(8,128)S(1)}, f32[3,3,72,256]{3,2,1,0:T(8,128)}, u32[]{:S(2)}, u32[]{:S(2)}) collective-permute-start(f32[3,3,72,256]{3,2,1,0:T(8,128)S(1)} %pad_maximum_fusion.4), channel_id=1, source_target_pairs={{0,1},{1,2},{2,3},{3,0},{4,5},{5,6},{6,7},{7,4},{8,9},{9,10},{10,1... | collective-permute-start | bytes 1990664 | tf_op jit(solution)/shard_map/ppermute | solution.py:453
  828.4 18.5 %collective-permute-start.3 = (f32[3,3,72,256]{3,2,1,0:T(8,128)S(1)}, f32[3,3,72,256]{3,2,1,0:T(8,128)}, u32[]{:S(2)}, u32[]{:S(2)}) collective-permute-start(f32[3,3,72,256]{3,2,1,0:T(8,128)S(1)} %pad_maximum_fusion.5), channel_id=1, source_target_pairs={{1,0},{2,1},{3,2},{0,3},{5,4},{6,5},{7,6},{4,7},{9,8},{10,9},{11,1... | collective-permute-start | bytes 1990664 | tf_op jit(solution)/shard_map/ppermute | solution.py:454
  831.6 15.3 %collective-permute-start.16 = (f32[68,16,80]{2,1,0:T(8,128)}, f32[68,16,80]{2,1,0:T(8,128)}, u32[]{:S(2)}, u32[]{:S(2)}) collective-permute-start(f32[68,16,80]{2,1,0:T(8,128)} %fusion), channel_id=1, source_target_pairs={{0,16},{1,17},{2,18},{3,19},{4,20},{5,21},{6,22},{7,23},{8,24},{9,... | collective-permute-start | bytes 1044488 | tf_op jit(solution)/shard_map/ppermute | solution.py:23
  (14 other events, 81.1 us)
